TPU v7x, 32 devices: a whole 2x2x4 slice. The times are simulated.
32 devices in a mesh: tx: 4 (over z), ty: 2 (over y), vel: 4 (over x, core).
Axes of the slice: x: 2, y: 2, z: 4, core: 2. Of those that a mesh axis runs over, the one named last changes fastest.
Arguments:
- initial: float32 [32, 16, 16, 3072], P('tx', 'ty', None, 'vel'), may hold values from -2 to 3.5
- velocity: float32 [3, 3072], P(None, 'vel'), may hold values from -3 to 3, as said below
- weights: float32 [3072], P('vel'), may hold values from 0.5 to 2
- wall: int32 [32, 16, 16], P('tx', 'ty'), may hold values 0 or 1
- wall_temp: float32 [32, 16, 16], P('tx', 'ty'), may hold values from -1 to 1
- mass_target: float32 [], replicated, may hold values from 0.5 to 1.5
Outputs:
- distribution: float32 [32, 16, 16, 3072], P('tx', 'ty', None, 'vel')
- macro_fields: float32 [5, 32, 16, 16], P(None, 'tx', 'ty')
Inputs may be any that keep to these rules, and one draw needn't show every extreme that they name: `velocity`: within each aligned block of 768 velocities the first quarter has positive x and y components, the second positive x and negative y, the third negative x and positive y, the fourth negative x and y; x and y components are 0.05 or more in magnitude.
All inputs are finite; a program needn't handle non-finite values. No bound on the sum of `wall` on one device may be relied on, other than what follows from the above.
Results may differ from a plain program's by a relative error of at most 0.0003.
Values sent between devices are 32-bit elements; how exact they have to be, the bound alone decides.
No kernel may reach another device: no remote copies, remote signals or barrier semaphores. Data moves between devices by JAX's collectives and lax.ppermute only.
A program may use at most 128 MiB of HBM per device.

v0:
```python
import jax
import jax.numpy as jnp
from jax import lax
from jax.sharding import PartitionSpec as P

ITERS = 3
MACRO_STEPS = 4
step_time = 0.1
collision = 1.0
macro_time = 0.1
viscosity = 1.0
conduction = 1.0
highest = lax.Precision.HIGHEST


def padded_2(cells, sides, width):
    for axis, dim in sides:
        count = lax.axis_size(axis)
        head = lax.slice_in_dim(cells, 0, width, axis=dim)
        tail = lax.slice_in_dim(cells, cells.shape[dim] - width, cells.shape[dim], axis=dim)
        cells = jnp.concatenate(
            [
                lax.ppermute(tail, axis, [(i, (i + 1) % count) for i in range(count)]),
                cells,
                lax.ppermute(head, axis, [((i + 1) % count, i) for i in range(count)]),
            ],
            axis=dim,
        )
    return cells


def basis(velocity):
    speed_sq = velocity[0] * velocity[0] + velocity[1] * velocity[1] + velocity[2] * velocity[2]
    return jnp.stack(
        [
            jnp.ones_like(speed_sq),
            2.0 * velocity[0],
            2.0 * velocity[1],
            2.0 * velocity[2],
            speed_sq - 1.5,
        ]
    )


def projector(velocity, weights, total_count):
    vel_x, vel_y, vel_z = (velocity[0], velocity[1], velocity[2])
    speed_sq = vel_x * vel_x + vel_y * vel_y + vel_z * vel_z
    moment_rows = jnp.stack(
        [
            jnp.ones_like(speed_sq),
            vel_x,
            vel_y,
            vel_z,
            2.0 / 3.0 * speed_sq - 1.0,
            2.0 * (vel_x * vel_x - speed_sq / 3.0),
            2.0 * (vel_y * vel_y - speed_sq / 3.0),
            2.0 * (vel_z * vel_z - speed_sq / 3.0),
            2.0 * vel_x * vel_y,
            2.0 * vel_x * vel_z,
            2.0 * vel_y * vel_z,
            vel_x * (speed_sq - 2.5),
            vel_y * (speed_sq - 2.5),
            vel_z * (speed_sq - 2.5),
        ]
    )
    return moment_rows * (weights / total_count)[None, :]


def differences(shifted):
    grads = [(shifted(direction, 1) - shifted(direction, -1)) * 0.5 for direction in (1, 2, 3)]
    middle = shifted(1, 0)
    laplace = (
        shifted(1, 1)
        + shifted(1, -1)
        - 2.0 * middle
        + (shifted(2, 1) + shifted(2, -1) - 2.0 * middle)
    )
    laplace = laplace + (shifted(3, 1) + shifted(3, -1) - 2.0 * middle)
    return (grads, laplace, middle)


def macro_sources(shifted):
    grads, laplace, middle = differences(shifted)
    grad_x, grad_y, grad_z = grads
    sig_x = grad_x[0] + grad_y[3] + grad_z[4]
    sig_y = grad_x[3] + grad_y[1] + grad_z[5]
    sig_z = grad_x[4] + grad_y[5] + grad_z[2]
    heat_flow = grad_x[6] + grad_y[7] + grad_z[8]
    return jnp.stack(
        [
            -0.5 * (sig_x + viscosity * laplace[9]),
            -0.5 * (sig_y + viscosity * laplace[10]),
            -0.5 * (sig_z + viscosity * laplace[11]),
            -(2.0 / 3.0) * (heat_flow + conduction * laplace[12]),
        ]
    )


def macro_step(shifted, sources):
    grads, laplace, middle = differences(shifted)
    grad_x, grad_y, grad_z = grads
    div_u = grad_x[1] + grad_y[2] + grad_z[3]
    change_rates = [-div_u]
    for component in range(3):
        along = grads[component]
        change_rates.append(
            -0.5 * (along[0] + along[4])
            + 0.5 * viscosity * laplace[1 + component]
            + sources[component]
        )
    change_rates.append(-(2.0 / 3.0) * div_u + 2.0 / 3.0 * conduction * laplace[4] + sources[3])
    return middle + macro_time * jnp.stack(change_rates)


def kinetic_update(corrected, equilibrium, before_x, after_x, before_y, after_y, velocity):
    plus_part = jnp.maximum(velocity, 0.0)
    minus_part = jnp.minimum(velocity, 0.0)
    before_z = jnp.roll(corrected, 1, 2)
    after_z = jnp.roll(corrected, -1, 2)
    transport = plus_part[0] * (corrected - before_x) + minus_part[0] * (after_x - corrected)
    transport = transport + (
        plus_part[1] * (corrected - before_y) + minus_part[1] * (after_y - corrected)
    )
    transport = transport + (
        plus_part[2] * (corrected - before_z) + minus_part[2] * (after_z - corrected)
    )
    return corrected - step_time * transport + step_time * collision * (equilibrium - corrected)


def padded_view(padded):

    def shifted(direction, offset):
        selector = [slice(None), slice(1, -1), slice(1, -1), slice(1, -1)]
        extent = padded.shape[direction]
        selector[direction] = slice(1 + offset, extent - 1 + offset)
        return padded[tuple(selector)]

    return shifted


def wrap_depth(padded):
    return jnp.concatenate([padded[..., -1:], padded, padded[..., :1]], axis=3)


def pad_sources(fields):
    padded = wrap_depth(padded_2(fields, (("tx", 1), ("ty", 2)), 1))
    return padded


def pad_state(macro_state):
    padded = wrap_depth(padded_2(macro_state, (("tx", 1), ("ty", 2)), 1))
    return padded


def total_mass(local_sum):
    summed = lax.psum(local_sum, ("tx", "ty"))
    return summed


def on_device(initial, velocity, weights, wall, wall_temp, mass_target):
    width_dev = weights.shape[0]
    total_velocities = float(width_dev * lax.axis_size("vel"))
    cell_count = float(
        wall.shape[0] * wall.shape[1] * wall.shape[2] * lax.axis_size("tx") * lax.axis_size("ty")
    )
    moment_rows = projector(velocity, weights, total_velocities)
    rows = basis(velocity)
    is_wall = (wall == 1)[..., None]
    wall_state = wall_temp[..., None] * rows[4]
    distribution = initial
    macro_state = None
    for iteration in range(ITERS):
        local_moments = jnp.einsum("kv,xyzv->kxyz", moment_rows, distribution, precision=highest)
        moments = lax.psum(local_moments, "vel")
        kinetic_state = moments[0:5]
        fields = jnp.concatenate([moments[5:14], moments[1:5]])
        mass_total = total_mass(jnp.sum(kinetic_state[0]))
        sources = macro_sources(padded_view(pad_sources(fields)))
        macro_state = kinetic_state
        for sweep in range(MACRO_STEPS):
            macro_state = macro_step(padded_view(pad_state(macro_state)), sources)
        density_mean = mass_total / cell_count
        macro_state = jnp.concatenate(
            [(macro_state[0] - density_mean + mass_target)[None], macro_state[1:]]
        )
        change = macro_state - kinetic_state
        corrected = distribution + jnp.einsum("kxyz,kv->xyzv", change, rows, precision=highest)
        equilibrium = jnp.einsum("kxyz,kv->xyzv", macro_state, rows, precision=highest)
        padded = padded_2(corrected, (("tx", 0), ("ty", 1)), 1)
        before_x = padded[:-2, 1:-1]
        after_x = padded[2:, 1:-1]
        before_y = padded[1:-1, :-2]
        after_y = padded[1:-1, 2:]
        updated = kinetic_update(
            corrected, equilibrium, before_x, after_x, before_y, after_y, velocity
        )
        distribution = jnp.where(is_wall, wall_state, updated)
    return (distribution, macro_state)


def solution(mesh):
    placed = (
        P("tx", "ty", None, "vel"),
        P(None, "vel"),
        P("vel"),
        P("tx", "ty", None),
        P("tx", "ty", None),
        P(),
    )
    return jax.shard_map(
        on_device,
        mesh=mesh,
        in_specs=placed,
        out_specs=(P("tx", "ty", None, "vel"), P(None, "tx", "ty", None)),
        check_vma=False,
    )
```

profile of v0, /device:TPU:0, one launch (start us, length us, event | category | flops | bytes accessed | tf_op | source)
XLA Modules:
  0.0 449.7 jit_solution(716490009049969232)
XLA Ops:
  4.4 12.9 %fusion.73 = f32[14,8,8,16]{3,0,2,1:T(8,128)S(1)} fusion(f32[8,8,16,768]{3,2,1,0:T(8,128)} %param.6, f32[14,768]{1,0:T(8,128)S(1)} %stack.29, f32[768]{0:T(1024)S(1)} %broadcast_multiply_fusion), kind=kOutput, calls=%fused_computation.583 | convolution fusion | flops 132131328 | bytes 3249152 | tf_op jit(solution)/shard_map/kv,xyzv->kxyz/dot_general | solution.py:173
  17.5 17.4 %psum.42 = f32[14,8,8,16]{3,2,1,0:T(8,128)S(1)} all-reduce(f32[14,8,8,16]{3,2,1,0:T(8,128)S(1)} %copy.9), channel_id=1, replica_groups=mesh['tx'=4,'ty'=2,'vel'=4] {'vel'}, use_global_device_ids=true, to_apply=%region_0.0 | all-reduce | flops 14336 | bytes 114688 | tf_op jit(solution)/shard_map/psum | solution.py:174
  36.5 2.2 collective-permute-start
  44.1 2.7 collective-permute-start.4
  51.1 2.2 collective-permute-done.7
  58.4 2.8 collective-permute-start.8
  70.0 2.8 collective-permute-start.12
  82.4 2.6 collective-permute-start.16
  89.4 21.9 %psum.43 = f32[]{:T(128)} all-reduce(f32[]{:T(128)} %slice_reduce_fusion.2), channel_id=1, replica_groups=mesh['tx'=4,'ty'=2,'vel'=4] {'tx','ty'}, use_global_device_ids=true, to_apply=%region_2.0 | all-reduce | flops 1 | bytes 8 | tf_op jit(solution)/shard_map/psum | solution.py:156
  114.7 2.8 convolution_add_fusion.2
  117.6 4.2 collective-permute-start.21
  122.0 5.3 %collective-permute-done.20 = f32[1,8,16,768]{3,2,1,0:T(8,128)S(1)} collective-permute-done((f32[1,8,16,768]{3,2,1,0:T(8,128)S(1)}, f32[1,8,16,768]{3,2,1,0:T(8,128)S(1)}, u32[]{:S(2)}, u32[]{:S(2)}) %collective-permute-start.20) | collective-permute-done | bytes 393248 | tf_op jit(solution)/shard_map/ppermute | solution.py:23
  127.3 2.8 collective-permute-done.21
  133.1 5.9 %collective-permute-done.22 = f32[10,1,16,768]{3,2,1,0:T(8,128)S(1)} collective-permute-done((f32[10,1,16,768]{3,2,1,0:T(8,128)S(1)}, f32[10,1,16,768]{3,2,1,0:T(8,128)S(1)}, u32[]{:S(2)}, u32[]{:S(2)}) %collective-permute-start.22) | collective-permute-done | bytes 491552 | tf_op jit(solution)/shard_map/ppermute | solution.py:23
  139.0 5.3 %collective-permute-done.23 = f32[10,1,16,768]{3,2,1,0:T(8,128)S(1)} collective-permute-done((f32[10,1,16,768]{3,2,1,0:T(8,128)S(1)}, f32[10,1,16,768]{3,2,1,0:T(8,128)S(1)}, u32[]{:S(2)}, u32[]{:S(2)}) %collective-permute-start.23) | collective-permute-done | bytes 491552 | tf_op jit(solution)/shard_map/ppermute | solution.py:25
  144.4 6.1 %multiply_select_fusion.2 = f32[8,8,16,768]{3,2,1,0:T(8,128)S(1)} fusion(f32[8,8,16,768]{3,2,1,0:T(8,128)S(1)} %convolution_add_fusion.2, f32[10,1,16,768]{3,2,1,0:T(8,128)S(1)} %collective-permute-done.23, f32[1,8,16,768]{3,2,1,0:T(8,128)S(1)} %collective-permute-done.21, f32[1,8,16,768]{3,2,1,0:T(8,128)S(1)} %collective-permute-done.20, ...), kind=kOutput, calls=%fused_computation.2 | convolution fusion | flops 73924608 | bytes 14414848 | tf_op jit(solution)/shard_map/kxyz,kv->xyzv/dot_general | solution.py:188
  150.5 11.2 %fusion.71 = f32[14,8,8,16]{3,0,2,1:T(8,128)S(1)} fusion(f32[8,8,16,768]{3,2,1,0:T(8,128)S(1)} %multiply_select_fusion.2, f32[14,768]{1,0:T(8,128)S(1)} %stack.29, f32[768]{0:T(1024)S(1)} %broadcast_multiply_fusion), kind=kOutput, calls=%fused_computation.581 | convolution fusion | flops 132131328 | bytes 3249152 | tf_op jit(solution)/shard_map/kv,xyzv->kxyz/dot_general | solution.py:173
  162.6 16.1 %psum.44 = f32[14,8,8,16]{3,2,1,0:T(8,128)} all-reduce(f32[14,8,8,16]{3,2,1,0:T(8,128)} %copy.12), channel_id=1, replica_groups=mesh['tx'=4,'ty'=2,'vel'=4] {'vel'}, use_global_device_ids=true, to_apply=%region_3.4 | all-reduce | flops 14336 | bytes 114688 | tf_op jit(solution)/shard_map/psum | solution.py:174
  180.5 2.8 collective-permute-start.24
  188.4 3.8 collective-permute-start.28
  196.5 2.2 collective-permute-done.31
  202.9 3.8 collective-permute-start.32
  216.0 2.8 collective-permute-start.36
  227.6 2.7 collective-permute-start.40
  236.3 22.7 %psum.45 = f32[]{:T(128)} all-reduce(f32[]{:T(128)} %slice_reduce_fusion.1), channel_id=1, replica_groups=mesh['tx'=4,'ty'=2,'vel'=4] {'tx','ty'}, use_global_device_ids=true, to_apply=%region_5.6 | all-reduce | flops 1 | bytes 8 | tf_op jit(solution)/shard_map/psum | solution.py:156
  264.9 2.8 convolution_add_fusion.1
  267.9 4.2 collective-permute-start.45
  272.1 5.5 %collective-permute-done.44 = f32[1,8,16,768]{3,2,1,0:T(8,128)S(1)} collective-permute-done((f32[1,8,16,768]{3,2,1,0:T(8,128)S(1)}, f32[1,8,16,768]{3,2,1,0:T(8,128)S(1)}, u32[]{:S(2)}, u32[]{:S(2)}) %collective-permute-start.44) | collective-permute-done | bytes 393248 | tf_op jit(solution)/shard_map/ppermute | solution.py:23
  277.5 2.8 collective-permute-done.45
  283.4 5.9 %collective-permute-done.46 = f32[10,1,16,768]{3,2,1,0:T(8,128)S(1)} collective-permute-done((f32[10,1,16,768]{3,2,1,0:T(8,128)S(1)}, f32[10,1,16,768]{3,2,1,0:T(8,128)S(1)}, u32[]{:S(2)}, u32[]{:S(2)}) %collective-permute-start.46) | collective-permute-done | bytes 491552 | tf_op jit(solution)/shard_map/ppermute | solution.py:23
  289.3 5.3 %collective-permute-done.47 = f32[10,1,16,768]{3,2,1,0:T(8,128)S(1)} collective-permute-done((f32[10,1,16,768]{3,2,1,0:T(8,128)S(1)}, f32[10,1,16,768]{3,2,1,0:T(8,128)S(1)}, u32[]{:S(2)}, u32[]{:S(2)}) %collective-permute-start.47) | collective-permute-done | bytes 491552 | tf_op jit(solution)/shard_map/ppermute | solution.py:25
  294.6 6.1 %multiply_select_fusion.1 = f32[8,8,16,768]{3,2,1,0:T(8,128)S(1)} fusion(f32[8,8,16,768]{3,2,1,0:T(8,128)S(1)} %convolution_add_fusion.1, f32[10,1,16,768]{3,2,1,0:T(8,128)S(1)} %collective-permute-done.47, f32[1,8,16,768]{3,2,1,0:T(8,128)S(1)} %collective-permute-done.45, f32[1,8,16,768]{3,2,1,0:T(8,128)S(1)} %collective-permute-done.44, ...), kind=kOutput, calls=%fused_computation.1 | convolution fusion | flops 73924608 | bytes 14414848 | tf_op jit(solution)/shard_map/kxyz,kv->xyzv/dot_general | solution.py:188
  300.8 11.2 %fusion.69 = f32[14,8,8,16]{3,0,2,1:T(8,128)S(1)} fusion(f32[8,8,16,768]{3,2,1,0:T(8,128)S(1)} %multiply_select_fusion.1, f32[14,768]{1,0:T(8,128)S(1)} %stack.29, f32[768]{0:T(1024)S(1)} %copy-done.6), kind=kOutput, calls=%fused_computation.579 | convolution fusion | flops 132131328 | bytes 3249152 | tf_op jit(solution)/shard_map/kv,xyzv->kxyz/dot_general | solution.py:173
  312.9 16.1 %psum.46 = f32[14,8,8,16]{3,2,1,0:T(8,128)} all-reduce(f32[14,8,8,16]{3,2,1,0:T(8,128)} %copy.15), channel_id=1, replica_groups=mesh['tx'=4,'ty'=2,'vel'=4] {'vel'}, use_global_device_ids=true, to_apply=%region_6.7 | all-reduce | flops 14336 | bytes 114688 | tf_op jit(solution)/shard_map/psum | solution.py:174
  329.7 3.8 collective-permute-start.48
  338.6 3.8 collective-permute-start.52
  346.8 2.2 collective-permute-done.55
  353.1 3.8 collective-permute-start.56
  366.2 2.8 collective-permute-start.60
  377.9 2.7 collective-permute-start.64
  386.5 22.9 %psum.47 = f32[]{:T(128)} all-reduce(f32[]{:T(128)} %slice_reduce_fusion), channel_id=1, replica_groups=mesh['tx'=4,'ty'=2,'vel'=4] {'tx','ty'}, use_global_device_ids=true, to_apply=%region_8.9 | all-reduce | flops 1 | bytes 8 | tf_op jit(solution)/shard_map/psum | solution.py:156
  412.3 2.8 convolution_add_fusion
  415.2 3.8 collective-permute-start.69
  419.0 5.9 %collective-permute-done.68 = f32[1,8,16,768]{3,2,1,0:T(8,128)S(1)} collective-permute-done((f32[1,8,16,768]{3,2,1,0:T(8,128)S(1)}, f32[1,8,16,768]{3,2,1,0:T(8,128)S(1)}, u32[]{:S(2)}, u32[]{:S(2)}) %collective-permute-start.68) | collective-permute-done | bytes 393248 | tf_op jit(solution)/shard_map/ppermute | solution.py:23
  424.9 2.4 collective-permute-done.69
  430.4 5.9 %collective-permute-done.70 = f32[10,1,16,768]{3,2,1,0:T(8,128)S(1)} collective-permute-done((f32[10,1,16,768]{3,2,1,0:T(8,128)S(1)}, f32[10,1,16,768]{3,2,1,0:T(8,128)S(1)}, u32[]{:S(2)}, u32[]{:S(2)}) %collective-permute-start.70) | collective-permute-done | bytes 491552 | tf_op jit(solution)/shard_map/ppermute | solution.py:23
  436.2 5.3 %collective-permute-done.71 = f32[10,1,16,768]{3,2,1,0:T(8,128)S(1)} collective-permute-done((f32[10,1,16,768]{3,2,1,0:T(8,128)S(1)}, f32[10,1,16,768]{3,2,1,0:T(8,128)S(1)}, u32[]{:S(2)}, u32[]{:S(2)}) %collective-permute-start.71) | collective-permute-done | bytes 491552 | tf_op jit(solution)/shard_map/ppermute | solution.py:25
  441.6 7.9 %multiply_select_fusion = f32[8,8,16,768]{3,2,1,0:T(8,128)} fusion(f32[8,8,16,768]{3,2,1,0:T(8,128)S(1)} %convolution_add_fusion, f32[10,1,16,768]{3,2,1,0:T(8,128)S(1)} %collective-permute-done.71, f32[1,8,16,768]{3,2,1,0:T(8,128)S(1)} %collective-permute-done.69, f32[1,8,16,768]{3,2,1,0:T(8,128)S(1)} %collective-permute-done.68, ...), kind=kOutput, calls=%fused_computation | convolution fusion | flops 73924608 | bytes 14414848 | tf_op jit(solution)/shard_map/kxyz,kv->xyzv/dot_general | solution.py:188
  (403 shorter events, 140.3 us)
Async XLA Ops:
  34.9 5.6 %collective-permute-start.1 = (f32[5,1,8,16]{3,2,1,0:T(8,128)S(1)}, f32[5,1,8,16]{3,2,1,0:T(8,128)S(1)}, u32[]{:S(2)}, u32[]{:S(2)}) collective-permute-start(f32[5,1,8,16]{3,2,1,0:T(8,128)S(1)} %get-tuple-element.84), channel_id=1, source_target_pairs={{0,8},{8,16},{16,24},{24,0},{1,9},{9,17},{17,25},{25,1},{2,10},{10... | collective-permute-start | bytes 7688 | tf_op jit(solution)/shard_map/ppermute | solution.py:23
  40.6 6.2 %collective-permute-start.3 = (f32[5,10,1,16]{3,2,1,0:T(1,128)S(1)}, f32[5,10,1,16]{3,2,1,0:T(1,128)S(1)}, u32[]{:S(2)}, u32[]{:S(2)}) collective-permute-start(f32[5,10,1,16]{3,2,1,0:T(1,128)S(1)} %get-tuple-element.162), channel_id=1, source_target_pairs={{0,4},{4,0},{1,5},{5,1},{2,6},{6,2},{3,7},{7,3},{8,12},{12,8},{9,1... | collective-permute-start | bytes 9608 | tf_op jit(solution)/shard_map/ppermute | solution.py:23
  42.2 4.6 %collective-permute-start.2 = (f32[5,10,1,16]{3,2,1,0:T(1,128)S(1)}, f32[5,10,1,16]{3,2,1,0:T(1,128)S(1)}, u32[]{:S(2)}, u32[]{:S(2)}) collective-permute-start(f32[5,10,1,16]{3,2,1,0:T(1,128)S(1)} %get-tuple-element.163), channel_id=1, source_target_pairs={{4,0},{0,4},{5,1},{1,5},{6,2},{2,6},{7,3},{3,7},{12,8},{8,12},{13,... | collective-permute-start | bytes 9608 | tf_op jit(solution)/shard_map/ppermute | solution.py:25
  42.7 6.1 %collective-permute-start.5 = (f32[13,1,8,16]{3,2,1,0:T(8,128)S(1)}, f32[13,1,8,16]{3,2,1,0:T(8,128)S(1)}, u32[]{:S(2)}, u32[]{:S(2)}) collective-permute-start(f32[13,1,8,16]{3,2,1,0:T(8,128)S(1)} %get-tuple-element.90), channel_id=1, source_target_pairs={{0,8},{8,16},{16,24},{24,0},{1,9},{9,17},{17,25},{25,1},{2,10},{10... | collective-permute-start | bytes 19976 | tf_op jit(solution)/shard_map/ppermute | solution.py:23
  44.1 4.9 %collective-permute-start.4 = (f32[13,1,8,16]{3,2,1,0:T(8,128)S(1)}, f32[13,1,8,16]{3,2,1,0:T(8,128)S(1)}, u32[]{:S(2)}, u32[]{:S(2)}) collective-permute-start(f32[13,1,8,16]{3,2,1,0:T(8,128)S(1)} %get-tuple-element.91), channel_id=1, source_target_pairs={{8,0},{16,8},{24,16},{0,24},{9,1},{17,9},{25,17},{1,25},{10,2},{18... | collective-permute-start | bytes 19976 | tf_op jit(solution)/shard_map/ppermute | solution.py:25
  57.3 5.6 %collective-permute-start.9 = (f32[5,1,8,16]{3,2,1,0:T(8,128)S(1)}, f32[5,1,8,16]{3,2,1,0:T(8,128)S(1)}, u32[]{:S(2)}, u32[]{:S(2)}) collective-permute-start(f32[5,1,8,16]{3,2,1,0:T(8,128)S(1)} %get-tuple-element.184), channel_id=1, source_target_pairs={{0,8},{8,16},{16,24},{24,0},{1,9},{9,17},{17,25},{25,1},{2,10},{10... | collective-permute-start | bytes 7688 | tf_op jit(solution)/shard_map/ppermute | solution.py:23
  68.7 5.8 %collective-permute-start.13 = (f32[5,1,8,16]{3,2,1,0:T(8,128)S(1)}, f32[5,1,8,16]{3,2,1,0:T(8,128)S(1)}, u32[]{:S(2)}, u32[]{:S(2)}) collective-permute-start(f32[5,1,8,16]{3,2,1,0:T(8,128)S(1)} %get-tuple-element.182), channel_id=1, source_target_pairs={{0,8},{8,16},{16,24},{24,0},{1,9},{9,17},{17,25},{25,1},{2,10},{10... | collective-permute-start | bytes 7688 | tf_op jit(solution)/shard_map/ppermute | solution.py:23
  80.9 5.7 %collective-permute-start.17 = (f32[5,1,8,16]{3,2,1,0:T(8,128)S(1)}, f32[5,1,8,16]{3,2,1,0:T(8,128)S(1)}, u32[]{:S(2)}, u32[]{:S(2)}) collective-permute-start(f32[5,1,8,16]{3,2,1,0:T(8,128)S(1)} %get-tuple-element.180), channel_id=1, source_target_pairs={{0,8},{8,16},{16,24},{24,0},{1,9},{9,17},{17,25},{25,1},{2,10},{10... | collective-permute-start | bytes 7688 | tf_op jit(solution)/shard_map/ppermute | solution.py:23
  86.7 25.9 %collective-permute-start.19 = (f32[5,10,1,16]{3,2,1,0:T(1,128)S(1)}, f32[5,10,1,16]{3,2,1,0:T(1,128)S(1)}, u32[]{:S(2)}, u32[]{:S(2)}) collective-permute-start(f32[5,10,1,16]{3,2,1,0:T(1,128)S(1)} %get-tuple-element.150), channel_id=1, source_target_pairs={{0,4},{4,0},{1,5},{5,1},{2,6},{6,2},{3,7},{7,3},{8,12},{12,8},{9,1... | collective-permute-start | bytes 9608 | tf_op jit(solution)/shard_map/ppermute | solution.py:23
  87.4 25.2 %collective-permute-start.18 = (f32[5,10,1,16]{3,2,1,0:T(1,128)S(1)}, f32[5,10,1,16]{3,2,1,0:T(1,128)S(1)}, u32[]{:S(2)}, u32[]{:S(2)}) collective-permute-start(f32[5,10,1,16]{3,2,1,0:T(1,128)S(1)} %get-tuple-element.151), channel_id=1, source_target_pairs={{4,0},{0,4},{5,1},{1,5},{6,2},{2,6},{7,3},{3,7},{12,8},{8,12},{13,... | collective-permute-start | bytes 9608 | tf_op jit(solution)/shard_map/ppermute | solution.py:25
  117.6 9.7 %collective-permute-start.20 = (f32[1,8,16,768]{3,2,1,0:T(8,128)S(1)}, f32[1,8,16,768]{3,2,1,0:T(8,128)S(1)}, u32[]{:S(2)}, u32[]{:S(2)}) collective-permute-start(f32[1,8,16,768]{3,2,1,0:T(8,128)S(1)} %get-tuple-element.60), channel_id=1, source_target_pairs={{0,8},{8,16},{16,24},{24,0},{1,9},{9,17},{17,25},{25,1},{2,10},{10... | collective-permute-start | bytes 1179656 | tf_op jit(solution)/shard_map/ppermute | solution.py:23
  117.6 12.4 %collective-permute-start.21 = (f32[1,8,16,768]{3,2,1,0:T(8,128)S(1)}, f32[1,8,16,768]{3,2,1,0:T(8,128)S(1)}, u32[]{:S(2)}, u32[]{:S(2)}) collective-permute-start(f32[1,8,16,768]{3,2,1,0:T(8,128)S(1)} %get-tuple-element.61), channel_id=1, source_target_pairs={{8,0},{16,8},{24,16},{0,24},{9,1},{17,9},{25,17},{1,25},{10,2},{18... | collective-permute-start | bytes 1179656 | tf_op jit(solution)/shard_map/ppermute | solution.py:25
  130.1 8.9 %collective-permute-start.22 = (f32[10,1,16,768]{3,2,1,0:T(8,128)S(1)}, f32[10,1,16,768]{3,2,1,0:T(8,128)S(1)}, u32[]{:S(2)}, u32[]{:S(2)}) collective-permute-start(f32[10,1,16,768]{3,2,1,0:T(8,128)S(1)} %get-tuple-element.42), channel_id=1, source_target_pairs={{0,4},{4,0},{1,5},{5,1},{2,6},{6,2},{3,7},{7,3},{8,12},{12,8},{9,1... | collective-permute-start | bytes 1474568 | tf_op jit(solution)/shard_map/ppermute | solution.py:23
  130.2 14.1 %collective-permute-start.23 = (f32[10,1,16,768]{3,2,1,0:T(8,128)S(1)}, f32[10,1,16,768]{3,2,1,0:T(8,128)S(1)}, u32[]{:S(2)}, u32[]{:S(2)}) collective-permute-start(f32[10,1,16,768]{3,2,1,0:T(8,128)S(1)} %get-tuple-element.43), channel_id=1, source_target_pairs={{4,0},{0,4},{5,1},{1,5},{6,2},{2,6},{7,3},{3,7},{12,8},{8,12},{13,... | collective-permute-start | bytes 1474568 | tf_op jit(solution)/shard_map/ppermute | solution.py:25
  179.5 6.7 %collective-permute-start.25 = (f32[5,1,8,16]{3,2,1,0:T(8,128)S(1)}, f32[5,1,8,16]{3,2,1,0:T(8,128)S(1)}, u32[]{:S(2)}, u32[]{:S(2)}) collective-permute-start(f32[5,1,8,16]{3,2,1,0:T(8,128)S(1)} %get-tuple-element.82), channel_id=1, source_target_pairs={{0,8},{8,16},{16,24},{24,0},{1,9},{9,17},{17,25},{25,1},{2,10},{10... | collective-permute-start | bytes 7688 | tf_op jit(solution)/shard_map/ppermute | solution.py:23
  180.5 5.6 %collective-permute-start.24 = (f32[5,1,8,16]{3,2,1,0:T(8,128)S(1)}, f32[5,1,8,16]{3,2,1,0:T(8,128)S(1)}, u32[]{:S(2)}, u32[]{:S(2)}) collective-permute-start(f32[5,1,8,16]{3,2,1,0:T(8,128)S(1)} %get-tuple-element.83), channel_id=1, source_target_pairs={{8,0},{16,8},{24,16},{0,24},{9,1},{17,9},{25,17},{1,25},{10,2},{18... | collective-permute-start | bytes 7688 | tf_op jit(solution)/shard_map/ppermute | solution.py:25
  186.2 6.0 %collective-permute-start.27 = (f32[5,10,1,16]{3,2,1,0:T(1,128)S(1)}, f32[5,10,1,16]{3,2,1,0:T(1,128)S(1)}, u32[]{:S(2)}, u32[]{:S(2)}) collective-permute-start(f32[5,10,1,16]{3,2,1,0:T(1,128)S(1)} %get-tuple-element.146), channel_id=1, source_target_pairs={{0,4},{4,0},{1,5},{5,1},{2,6},{6,2},{3,7},{7,3},{8,12},{12,8},{9,1... | collective-permute-start | bytes 9608 | tf_op jit(solution)/shard_map/ppermute | solution.py:23
  186.3 5.9 %collective-permute-start.26 = (f32[5,10,1,16]{3,2,1,0:T(1,128)S(1)}, f32[5,10,1,16]{3,2,1,0:T(1,128)S(1)}, u32[]{:S(2)}, u32[]{:S(2)}) collective-permute-start(f32[5,10,1,16]{3,2,1,0:T(1,128)S(1)} %get-tuple-element.147), channel_id=1, source_target_pairs={{4,0},{0,4},{5,1},{1,5},{6,2},{2,6},{7,3},{3,7},{12,8},{8,12},{13,... | collective-permute-start | bytes 9608 | tf_op jit(solution)/shard_map/ppermute | solution.py:25
  188.3 6.0 %collective-permute-start.29 = (f32[13,1,8,16]{3,2,1,0:T(8,128)S(1)}, f32[13,1,8,16]{3,2,1,0:T(8,128)S(1)}, u32[]{:S(2)}, u32[]{:S(2)}) collective-permute-start(f32[13,1,8,16]{3,2,1,0:T(8,128)S(1)} %get-tuple-element.88), channel_id=1, source_target_pairs={{0,8},{8,16},{16,24},{24,0},{1,9},{9,17},{17,25},{25,1},{2,10},{10... | collective-permute-start | bytes 19976 | tf_op jit(solution)/shard_map/ppermute | solution.py:23
  188.4 6.0 %collective-permute-start.28 = (f32[13,1,8,16]{3,2,1,0:T(8,128)S(1)}, f32[13,1,8,16]{3,2,1,0:T(8,128)S(1)}, u32[]{:S(2)}, u32[]{:S(2)}) collective-permute-start(f32[13,1,8,16]{3,2,1,0:T(8,128)S(1)} %get-tuple-element.89), channel_id=1, source_target_pairs={{8,0},{16,8},{24,16},{0,24},{9,1},{17,9},{25,17},{1,25},{10,2},{18... | collective-permute-start | bytes 19976 | tf_op jit(solution)/shard_map/ppermute | solution.py:25
  194.6 4.9 %collective-permute-start.30 = (f32[13,10,1,16]{3,2,1,0:T(1,128)S(1)}, f32[13,10,1,16]{3,2,1,0:T(1,128)S(1)}, u32[]{:S(2)}, u32[]{:S(2)}) collective-permute-start(f32[13,10,1,16]{3,2,1,0:T(1,128)S(1)} %get-tuple-element.75), channel_id=1, source_target_pairs={{4,0},{0,4},{5,1},{1,5},{6,2},{2,6},{7,3},{3,7},{12,8},{8,12},{13,... | collective-permute-start | bytes 24968 | tf_op jit(solution)/shard_map/ppermute | solution.py:25
  202.8 5.6 %collective-permute-start.33 = (f32[5,1,8,16]{3,2,1,0:T(8,128)S(1)}, f32[5,1,8,16]{3,2,1,0:T(8,128)S(1)}, u32[]{:S(2)}, u32[]{:S(2)}) collective-permute-start(f32[5,1,8,16]{3,2,1,0:T(8,128)S(1)} %get-tuple-element.176), channel_id=1, source_target_pairs={{0,8},{8,16},{16,24},{24,0},{1,9},{9,17},{17,25},{25,1},{2,10},{10... | collective-permute-start | bytes 7688 | tf_op jit(solution)/shard_map/ppermute | solution.py:23
  202.9 5.6 %collective-permute-start.32 = (f32[5,1,8,16]{3,2,1,0:T(8,128)S(1)}, f32[5,1,8,16]{3,2,1,0:T(8,128)S(1)}, u32[]{:S(2)}, u32[]{:S(2)}) collective-permute-start(f32[5,1,8,16]{3,2,1,0:T(8,128)S(1)} %get-tuple-element.177), channel_id=1, source_target_pairs={{8,0},{16,8},{24,16},{0,24},{9,1},{17,9},{25,17},{1,25},{10,2},{18... | collective-permute-start | bytes 7688 | tf_op jit(solution)/shard_map/ppermute | solution.py:25
  214.8 5.7 %collective-permute-start.37 = (f32[5,1,8,16]{3,2,1,0:T(8,128)S(1)}, f32[5,1,8,16]{3,2,1,0:T(8,128)S(1)}, u32[]{:S(2)}, u32[]{:S(2)}) collective-permute-start(f32[5,1,8,16]{3,2,1,0:T(8,128)S(1)} %get-tuple-element.174), channel_id=1, source_target_pairs={{0,8},{8,16},{16,24},{24,0},{1,9},{9,17},{17,25},{25,1},{2,10},{10... | collective-permute-start | bytes 7688 | tf_op jit(solution)/shard_map/ppermute | solution.py:23
  226.5 5.7 %collective-permute-start.41 = (f32[5,1,8,16]{3,2,1,0:T(8,128)S(1)}, f32[5,1,8,16]{3,2,1,0:T(8,128)S(1)}, u32[]{:S(2)}, u32[]{:S(2)}) collective-permute-start(f32[5,1,8,16]{3,2,1,0:T(8,128)S(1)} %get-tuple-element.172), channel_id=1, source_target_pairs={{0,8},{8,16},{16,24},{24,0},{1,9},{9,17},{17,25},{25,1},{2,10},{10... | collective-permute-start | bytes 7688 | tf_op jit(solution)/shard_map/ppermute | solution.py:23
  232.8 26.8 %collective-permute-start.43 = (f32[5,10,1,16]{3,2,1,0:T(1,128)}, f32[5,10,1,16]{3,2,1,0:T(1,128)}, u32[]{:S(2)}, u32[]{:S(2)}) collective-permute-start(f32[5,10,1,16]{3,2,1,0:T(1,128)} %get-tuple-element.134), channel_id=1, source_target_pairs={{0,4},{4,0},{1,5},{5,1},{2,6},{6,2},{3,7},{7,3},{8,12},{12,8},{9,1... | collective-permute-start | bytes 9608 | tf_op jit(solution)/shard_map/ppermute | solution.py:23
  234.2 25.5 %collective-permute-start.42 = (f32[5,10,1,16]{3,2,1,0:T(1,128)}, f32[5,10,1,16]{3,2,1,0:T(1,128)}, u32[]{:S(2)}, u32[]{:S(2)}) collective-permute-start(f32[5,10,1,16]{3,2,1,0:T(1,128)} %get-tuple-element.135), channel_id=1, source_target_pairs={{4,0},{0,4},{5,1},{1,5},{6,2},{2,6},{7,3},{3,7},{12,8},{8,12},{13,... | collective-permute-start | bytes 9608 | tf_op jit(solution)/shard_map/ppermute | solution.py:25
  267.8 9.7 %collective-permute-start.44 = (f32[1,8,16,768]{3,2,1,0:T(8,128)S(1)}, f32[1,8,16,768]{3,2,1,0:T(8,128)S(1)}, u32[]{:S(2)}, u32[]{:S(2)}) collective-permute-start(f32[1,8,16,768]{3,2,1,0:T(8,128)S(1)} %get-tuple-element.54), channel_id=1, source_target_pairs={{0,8},{8,16},{16,24},{24,0},{1,9},{9,17},{17,25},{25,1},{2,10},{10... | collective-permute-start | bytes 1179656 | tf_op jit(solution)/shard_map/ppermute | solution.py:23
  267.9 12.4 %collective-permute-start.45 = (f32[1,8,16,768]{3,2,1,0:T(8,128)S(1)}, f32[1,8,16,768]{3,2,1,0:T(8,128)S(1)}, u32[]{:S(2)}, u32[]{:S(2)}) collective-permute-start(f32[1,8,16,768]{3,2,1,0:T(8,128)S(1)} %get-tuple-element.55), channel_id=1, source_target_pairs={{8,0},{16,8},{24,16},{0,24},{9,1},{17,9},{25,17},{1,25},{10,2},{18... | collective-permute-start | bytes 1179656 | tf_op jit(solution)/shard_map/ppermute | solution.py:25
  280.4 8.9 %collective-permute-start.46 = (f32[10,1,16,768]{3,2,1,0:T(8,128)S(1)}, f32[10,1,16,768]{3,2,1,0:T(8,128)S(1)}, u32[]{:S(2)}, u32[]{:S(2)}) collective-permute-start(f32[10,1,16,768]{3,2,1,0:T(8,128)S(1)} %get-tuple-element.40), channel_id=1, source_target_pairs={{0,4},{4,0},{1,5},{5,1},{2,6},{6,2},{3,7},{7,3},{8,12},{12,8},{9,1... | collective-permute-start | bytes 1474568 | tf_op jit(solution)/shard_map/ppermute | solution.py:23
  280.5 14.1 %collective-permute-start.47 = (f32[10,1,16,768]{3,2,1,0:T(8,128)S(1)}, f32[10,1,16,768]{3,2,1,0:T(8,128)S(1)}, u32[]{:S(2)}, u32[]{:S(2)}) collective-permute-start(f32[10,1,16,768]{3,2,1,0:T(8,128)S(1)} %get-tuple-element.41), channel_id=1, source_target_pairs={{4,0},{0,4},{5,1},{1,5},{6,2},{2,6},{7,3},{3,7},{12,8},{8,12},{13,... | collective-permute-start | bytes 1474568 | tf_op jit(solution)/shard_map/ppermute | solution.py:25
  329.7 6.7 %collective-permute-start.49 = (f32[5,1,8,16]{3,2,1,0:T(8,128)S(1)}, f32[5,1,8,16]{3,2,1,0:T(8,128)S(1)}, u32[]{:S(2)}, u32[]{:S(2)}) collective-permute-start(f32[5,1,8,16]{3,2,1,0:T(8,128)S(1)} %get-tuple-element.80), channel_id=1, source_target_pairs={{0,8},{8,16},{16,24},{24,0},{1,9},{9,17},{17,25},{25,1},{2,10},{10... | collective-permute-start | bytes 7688 | tf_op jit(solution)/shard_map/ppermute | solution.py:23
  329.7 6.7 %collective-permute-start.48 = (f32[5,1,8,16]{3,2,1,0:T(8,128)S(1)}, f32[5,1,8,16]{3,2,1,0:T(8,128)S(1)}, u32[]{:S(2)}, u32[]{:S(2)}) collective-permute-start(f32[5,1,8,16]{3,2,1,0:T(8,128)S(1)} %get-tuple-element.81), channel_id=1, source_target_pairs={{8,0},{16,8},{24,16},{0,24},{9,1},{17,9},{25,17},{1,25},{10,2},{18... | collective-permute-start | bytes 7688 | tf_op jit(solution)/shard_map/ppermute | solution.py:25
  336.5 6.0 %collective-permute-start.51 = (f32[5,10,1,16]{3,2,1,0:T(1,128)S(1)}, f32[5,10,1,16]{3,2,1,0:T(1,128)S(1)}, u32[]{:S(2)}, u32[]{:S(2)}) collective-permute-start(f32[5,10,1,16]{3,2,1,0:T(1,128)S(1)} %get-tuple-element.130), channel_id=1, source_target_pairs={{0,4},{4,0},{1,5},{5,1},{2,6},{6,2},{3,7},{7,3},{8,12},{12,8},{9,1... | collective-permute-start | bytes 9608 | tf_op jit(solution)/shard_map/ppermute | solution.py:23
  336.5 5.9 %collective-permute-start.50 = (f32[5,10,1,16]{3,2,1,0:T(1,128)S(1)}, f32[5,10,1,16]{3,2,1,0:T(1,128)S(1)}, u32[]{:S(2)}, u32[]{:S(2)}) collective-permute-start(f32[5,10,1,16]{3,2,1,0:T(1,128)S(1)} %get-tuple-element.131), channel_id=1, source_target_pairs={{4,0},{0,4},{5,1},{1,5},{6,2},{2,6},{7,3},{3,7},{12,8},{8,12},{13,... | collective-permute-start | bytes 9608 | tf_op jit(solution)/shard_map/ppermute | solution.py:25
  338.6 6.0 %collective-permute-start.53 = (f32[13,1,8,16]{3,2,1,0:T(8,128)S(1)}, f32[13,1,8,16]{3,2,1,0:T(8,128)S(1)}, u32[]{:S(2)}, u32[]{:S(2)}) collective-permute-start(f32[13,1,8,16]{3,2,1,0:T(8,128)S(1)} %get-tuple-element.86), channel_id=1, source_target_pairs={{0,8},{8,16},{16,24},{24,0},{1,9},{9,17},{17,25},{25,1},{2,10},{10... | collective-permute-start | bytes 19976 | tf_op jit(solution)/shard_map/ppermute | solution.py:23
  338.6 6.0 %collective-permute-start.52 = (f32[13,1,8,16]{3,2,1,0:T(8,128)S(1)}, f32[13,1,8,16]{3,2,1,0:T(8,128)S(1)}, u32[]{:S(2)}, u32[]{:S(2)}) collective-permute-start(f32[13,1,8,16]{3,2,1,0:T(8,128)S(1)} %get-tuple-element.87), channel_id=1, source_target_pairs={{8,0},{16,8},{24,16},{0,24},{9,1},{17,9},{25,17},{1,25},{10,2},{18... | collective-permute-start | bytes 19976 | tf_op jit(solution)/shard_map/ppermute | solution.py:25
  344.8 4.9 %collective-permute-start.54 = (f32[13,10,1,16]{3,2,1,0:T(1,128)S(1)}, f32[13,10,1,16]{3,2,1,0:T(1,128)S(1)}, u32[]{:S(2)}, u32[]{:S(2)}) collective-permute-start(f32[13,10,1,16]{3,2,1,0:T(1,128)S(1)} %get-tuple-element.71), channel_id=1, source_target_pairs={{4,0},{0,4},{5,1},{1,5},{6,2},{2,6},{7,3},{3,7},{12,8},{8,12},{13,... | collective-permute-start | bytes 24968 | tf_op jit(solution)/shard_map/ppermute | solution.py:25
  353.1 5.6 %collective-permute-start.57 = (f32[5,1,8,16]{3,2,1,0:T(8,128)S(1)}, f32[5,1,8,16]{3,2,1,0:T(8,128)S(1)}, u32[]{:S(2)}, u32[]{:S(2)}) collective-permute-start(f32[5,1,8,16]{3,2,1,0:T(8,128)S(1)} %get-tuple-element.168), channel_id=1, source_target_pairs={{0,8},{8,16},{16,24},{24,0},{1,9},{9,17},{17,25},{25,1},{2,10},{10... | collective-permute-start | bytes 7688 | tf_op jit(solution)/shard_map/ppermute | solution.py:23
  353.1 5.6 %collective-permute-start.56 = (f32[5,1,8,16]{3,2,1,0:T(8,128)S(1)}, f32[5,1,8,16]{3,2,1,0:T(8,128)S(1)}, u32[]{:S(2)}, u32[]{:S(2)}) collective-permute-start(f32[5,1,8,16]{3,2,1,0:T(8,128)S(1)} %get-tuple-element.169), channel_id=1, source_target_pairs={{8,0},{16,8},{24,16},{0,24},{9,1},{17,9},{25,17},{1,25},{10,2},{18... | collective-permute-start | bytes 7688 | tf_op jit(solution)/shard_map/ppermute | solution.py:25
  365.1 5.7 %collective-permute-start.61 = (f32[5,1,8,16]{3,2,1,0:T(8,128)S(1)}, f32[5,1,8,16]{3,2,1,0:T(8,128)S(1)}, u32[]{:S(2)}, u32[]{:S(2)}) collective-permute-start(f32[5,1,8,16]{3,2,1,0:T(8,128)S(1)} %get-tuple-element.166), channel_id=1, source_target_pairs={{0,8},{8,16},{16,24},{24,0},{1,9},{9,17},{17,25},{25,1},{2,10},{10... | collective-permute-start | bytes 7688 | tf_op jit(solution)/shard_map/ppermute | solution.py:23
  376.8 5.6 %collective-permute-start.65 = (f32[5,1,8,16]{3,2,1,0:T(8,128)S(1)}, f32[5,1,8,16]{3,2,1,0:T(8,128)S(1)}, u32[]{:S(2)}, u32[]{:S(2)}) collective-permute-start(f32[5,1,8,16]{3,2,1,0:T(8,128)S(1)} %get-tuple-element.164), channel_id=1, source_target_pairs={{0,8},{8,16},{16,24},{24,0},{1,9},{9,17},{17,25},{25,1},{2,10},{10... | collective-permute-start | bytes 7688 | tf_op jit(solution)/shard_map/ppermute | solution.py:23
  383.1 27.1 %collective-permute-start.67 = (f32[5,10,1,16]{3,2,1,0:T(1,128)}, f32[5,10,1,16]{3,2,1,0:T(1,128)S(1)}, u32[]{:S(2)}, u32[]{:S(2)}) collective-permute-start(f32[5,10,1,16]{3,2,1,0:T(1,128)} %get-tuple-element.118), channel_id=1, source_target_pairs={{0,4},{4,0},{1,5},{5,1},{2,6},{6,2},{3,7},{7,3},{8,12},{12,8},{9,1... | collective-permute-start | bytes 9608 | tf_op jit(solution)/shard_map/ppermute | solution.py:23
  384.4 25.7 %collective-permute-start.66 = (f32[5,10,1,16]{3,2,1,0:T(1,128)}, f32[5,10,1,16]{3,2,1,0:T(1,128)S(1)}, u32[]{:S(2)}, u32[]{:S(2)}) collective-permute-start(f32[5,10,1,16]{3,2,1,0:T(1,128)} %get-tuple-element.119), channel_id=1, source_target_pairs={{4,0},{0,4},{5,1},{1,5},{6,2},{2,6},{7,3},{3,7},{12,8},{8,12},{13,... | collective-permute-start | bytes 9608 | tf_op jit(solution)/shard_map/ppermute | solution.py:25
  415.2 9.7 %collective-permute-start.68 = (f32[1,8,16,768]{3,2,1,0:T(8,128)S(1)}, f32[1,8,16,768]{3,2,1,0:T(8,128)S(1)}, u32[]{:S(2)}, u32[]{:S(2)}) collective-permute-start(f32[1,8,16,768]{3,2,1,0:T(8,128)S(1)} %get-tuple-element.48), channel_id=1, source_target_pairs={{0,8},{8,16},{16,24},{24,0},{1,9},{9,17},{17,25},{25,1},{2,10},{10... | collective-permute-start | bytes 1179656 | tf_op jit(solution)/shard_map/ppermute | solution.py:23
  415.2 12.0 %collective-permute-start.69 = (f32[1,8,16,768]{3,2,1,0:T(8,128)S(1)}, f32[1,8,16,768]{3,2,1,0:T(8,128)S(1)}, u32[]{:S(2)}, u32[]{:S(2)}) collective-permute-start(f32[1,8,16,768]{3,2,1,0:T(8,128)S(1)} %get-tuple-element.49), channel_id=1, source_target_pairs={{8,0},{16,8},{24,16},{0,24},{9,1},{17,9},{25,17},{1,25},{10,2},{18... | collective-permute-start | bytes 1179656 | tf_op jit(solution)/shard_map/ppermute | solution.py:25
  427.3 8.9 %collective-permute-start.70 = (f32[10,1,16,768]{3,2,1,0:T(8,128)S(1)}, f32[10,1,16,768]{3,2,1,0:T(8,128)S(1)}, u32[]{:S(2)}, u32[]{:S(2)}) collective-permute-start(f32[10,1,16,768]{3,2,1,0:T(8,128)S(1)} %get-tuple-element.38), channel_id=1, source_target_pairs={{0,4},{4,0},{1,5},{5,1},{2,6},{6,2},{3,7},{7,3},{8,12},{12,8},{9,1... | collective-permute-start | bytes 1474568 | tf_op jit(solution)/shard_map/ppermute | solution.py:23
  427.4 14.1 %collective-permute-start.71 = (f32[10,1,16,768]{3,2,1,0:T(8,128)S(1)}, f32[10,1,16,768]{3,2,1,0:T(8,128)S(1)}, u32[]{:S(2)}, u32[]{:S(2)}) collective-permute-start(f32[10,1,16,768]{3,2,1,0:T(8,128)S(1)} %get-tuple-element.39), channel_id=1, source_target_pairs={{4,0},{0,4},{5,1},{1,5},{6,2},{2,6},{7,3},{3,7},{12,8},{8,12},{13,... | collective-permute-start | bytes 1474568 | tf_op jit(solution)/shard_map/ppermute | solution.py:25
  (59 other events, 877.1 us)
where the time goes:
time: 457 us; the launch traced here: 450 us
  blocking collectives  117 us (26%)
  starting transfers between devices  109 us (24%)
  waiting for transfers between devices  106 us (23%)
  matrix products  63.9 us (14%)
  other arithmetic  31.8 us (7%)
  local copies, waits for them, and re-layouts  17.1 us (4%)
  between operations  5.41 us (1%)
    ppermute x36, starting transfers between devices, padded_2(): lax.ppermute(head, axis, [((i + 1) % count, i) for i in range(count)])  82.2 us
    ppermute x36, waiting for transfers between devices, padded_2(): lax.ppermute(tail, axis, [(i, (i + 1) % count) for i in range(count)])  72.4 us
    psum x3, blocking collectives, total_mass(): summed = lax.psum(local_sum, ('tx', 'ty'))  67.4 us
    psum x3, blocking collectives, on_device(): moments = lax.psum(local_moments, 'vel')  49.5 us
    dot_general x3, matrix products, on_device(): jnp.einsum('kv,xyzv->kxyz', moment_rows, distribution, precision=highest)  35.4 us
    ppermute x36, waiting for transfers between devices, padded_2(): lax.ppermute(head, axis, [((i + 1) % count, i) for i in range(count)])  33.4 us
    ppermute x36, starting transfers between devices, padded_2(): lax.ppermute(tail, axis, [(i, (i + 1) % count) for i in range(count)])  26.5 us
    dot_general x3, matrix products, on_device(): jnp.einsum('kxyz,kv->xyzv', macro_state, rows, precision=highest)  20.1 us
  transfers between devices with their start and end apart: 72, of which 44 were waited for; matrix products, arithmetic and copies ran while one was open for 3% of the time, Pallas kernels for 0%

commit v1 on v0

--- a/solution.py
+++ b/solution.py
@@ -171,7 +171,9 @@
     macro_state = None
     for iteration in range(ITERS):
         local_moments = jnp.einsum("kv,xyzv->kxyz", moment_rows, distribution, precision=highest)
-        moments = lax.psum(local_moments, "vel")
+        moments = local_moments
+        for hop in (1, 2):
+            moments = moments + lax.ppermute(moments, "vel", [(dev, dev ^ hop) for dev in range(4)])
         kinetic_state = moments[0:5]
         fields = jnp.concatenate([moments[5:14], moments[1:5]])
         mass_total = total_mass(jnp.sum(kinetic_state[0]))

time: 457 us -> 443 us (0.969)
  blocking collectives: 117 us -> 67.2 us
  waiting for transfers between devices: 106 us -> 146 us
  local copies, waits for them, and re-layouts: 17.1 us -> 8.55 us
  starting transfers between devices: 109 us -> 116 us
    psum x3 -> x0, blocking collectives: 49.5 us -> none  [on_device(): moments = lax.psum(local_moments, 'vel')]
    ppermute x0 -> x6, waiting for transfers between devices: none -> 38 us  [on_device(): lax.ppermute(moments, 'vel', [(dev, dev ^ hop) for dev in range(4)])]
    ppermute x0 -> x6, starting transfers between devices: none -> 6.72 us  [on_device(): lax.ppermute(moments, 'vel', [(dev, dev ^ hop) for dev in range(4)])]
    ppermute x36, starting transfers between devices: 26.5 us -> 31.6 us  [padded_2(): lax.ppermute(tail, axis, [(i, (i + 1) % count) for i in range(count)])]
  transfers between devices with their start and end apart: 72 -> 78, of which waited for: 44 -> 52; matrix products, arithmetic and copies ran while one was open for 3% -> 2% of each run, Pallas kernels for 0% -> 0%
where the time goes in v1:
time: 443 us; the launch traced here: 436 us
  waiting for transfers between devices  146 us (33%)
  starting transfers between devices  116 us (26%)
  blocking collectives  67.2 us (15%)
  matrix products  63.9 us (14%)
  other arithmetic  29 us (7%)
  local copies, waits for them, and re-layouts  8.55 us (2%)
  between operations  5.41 us (1%)
    ppermute x36, starting transfers between devices, padded_2(): lax.ppermute(head, axis, [((i + 1) % count, i) for i in range(count)])  77.9 us
    ppermute x36, waiting for transfers between devices, padded_2(): lax.ppermute(tail, axis, [(i, (i + 1) % count) for i in range(count)])  75.1 us
    psum x3, blocking collectives, total_mass(): summed = lax.psum(local_sum, ('tx', 'ty'))  67.2 us
    ppermute x6, waiting for transfers between devices, on_device(): lax.ppermute(moments, 'vel', [(dev, dev ^ hop) for dev in range(4)])  38 us
    dot_general x3, matrix products, on_device(): jnp.einsum('kv,xyzv->kxyz', moment_rows, distribution, precision=highest)  35.4 us
    ppermute x36, waiting for transfers between devices, padded_2(): lax.ppermute(head, axis, [((i + 1) % count, i) for i in range(count)])  32.9 us
    ppermute x36, starting transfers between devices, padded_2(): lax.ppermute(tail, axis, [(i, (i + 1) % count) for i in range(count)])  31.6 us
    dot_general x3, matrix products, on_device(): jnp.einsum('kxyz,kv->xyzv', macro_state, rows, precision=highest)  20.1 us
  transfers between devices with their start and end apart: 78, of which 52 were waited for; matrix products, arithmetic and copies ran while one was open for 2% of the time, Pallas kernels for 0%

profile of v1, /device:TPU:0, one launch (start us, length us, event | category | flops | bytes accessed | tf_op | source)
XLA Modules:
  0.0 436.3 jit_solution(3835065429991033864)
XLA Ops:
  4.4 12.9 %fusion.73 = f32[14,8,8,16]{3,0,2,1:T(8,128)S(1)} fusion(f32[8,8,16,768]{3,2,1,0:T(8,128)} %param.6, f32[14,768]{1,0:T(8,128)S(1)} %stack.29, f32[768]{0:T(1024)S(1)} %broadcast_multiply_fusion), kind=kOutput, calls=%fused_computation.583 | convolution fusion | flops 132131328 | bytes 3249152 | tf_op jit(solution)/shard_map/kv,xyzv->kxyz/dot_general | solution.py:173
  19.7 2.9 collective-permute-start.1
  22.6 10.8 %collective-permute-done.1 = f32[14,8,8,16]{3,2,1,0:T(8,128)S(1)} collective-permute-done((f32[14,8,8,16]{3,2,1,0:T(8,128)S(1)}, f32[14,8,8,16]{3,2,1,0:T(8,128)S(1)}, u32[]{:S(2)}, u32[]{:S(2)}) %collective-permute-start.1) | collective-permute-done | bytes 57376 | tf_op jit(solution)/shard_map/ppermute | solution.py:176
  42.9 2.6 collective-permute-start.6
  50.0 2.2 collective-permute-done.9
  57.2 2.8 collective-permute-start.10
  68.8 2.7 collective-permute-start.14
  81.2 2.4 collective-permute-start.18
  88.1 22.0 %psum.21 = f32[]{:T(128)} all-reduce(f32[]{:T(128)} %slice_reduce_fusion.2), channel_id=1, replica_groups=mesh['tx'=4,'ty'=2,'vel'=4] {'tx','ty'}, use_global_device_ids=true, to_apply=%region_1.0 | all-reduce | flops 1 | bytes 8 | tf_op jit(solution)/shard_map/psum | solution.py:156
  112.8 2.8 convolution_add_fusion.2
  115.7 4.2 collective-permute-start.23
  120.1 5.3 %collective-permute-done.22 = f32[1,8,16,768]{3,2,1,0:T(8,128)S(1)} collective-permute-done((f32[1,8,16,768]{3,2,1,0:T(8,128)S(1)}, f32[1,8,16,768]{3,2,1,0:T(8,128)S(1)}, u32[]{:S(2)}, u32[]{:S(2)}) %collective-permute-start.22) | collective-permute-done | bytes 393248 | tf_op jit(solution)/shard_map/ppermute | solution.py:23
  125.4 2.8 collective-permute-done.23
  131.2 5.9 %collective-permute-done.24 = f32[10,1,16,768]{3,2,1,0:T(8,128)S(1)} collective-permute-done((f32[10,1,16,768]{3,2,1,0:T(8,128)S(1)}, f32[10,1,16,768]{3,2,1,0:T(8,128)S(1)}, u32[]{:S(2)}, u32[]{:S(2)}) %collective-permute-start.24) | collective-permute-done | bytes 491552 | tf_op jit(solution)/shard_map/ppermute | solution.py:23
  137.1 5.3 %collective-permute-done.25 = f32[10,1,16,768]{3,2,1,0:T(8,128)S(1)} collective-permute-done((f32[10,1,16,768]{3,2,1,0:T(8,128)S(1)}, f32[10,1,16,768]{3,2,1,0:T(8,128)S(1)}, u32[]{:S(2)}, u32[]{:S(2)}) %collective-permute-start.25) | collective-permute-done | bytes 491552 | tf_op jit(solution)/shard_map/ppermute | solution.py:25
  142.5 6.1 %multiply_select_fusion.2 = f32[8,8,16,768]{3,2,1,0:T(8,128)S(1)} fusion(f32[8,8,16,768]{3,2,1,0:T(8,128)S(1)} %convolution_add_fusion.2, f32[10,1,16,768]{3,2,1,0:T(8,128)S(1)} %collective-permute-done.25, f32[1,8,16,768]{3,2,1,0:T(8,128)S(1)} %collective-permute-done.23, f32[1,8,16,768]{3,2,1,0:T(8,128)S(1)} %collective-permute-done.22, ...), kind=kOutput, calls=%fused_computation.2 | convolution fusion | flops 73924608 | bytes 14414848 | tf_op jit(solution)/shard_map/kxyz,kv->xyzv/dot_general | solution.py:190
  148.6 11.2 %fusion.71 = f32[14,8,8,16]{3,0,2,1:T(8,128)S(1)} fusion(f32[8,8,16,768]{3,2,1,0:T(8,128)S(1)} %multiply_select_fusion.2, f32[14,768]{1,0:T(8,128)S(1)} %stack.29, f32[768]{0:T(1024)S(1)} %broadcast_multiply_fusion), kind=kOutput, calls=%fused_computation.581 | convolution fusion | flops 132131328 | bytes 3249152 | tf_op jit(solution)/shard_map/kv,xyzv->kxyz/dot_general | solution.py:173
  163.6 11.1 %collective-permute-done.27 = f32[14,8,8,16]{3,2,1,0:T(8,128)S(1)} collective-permute-done((f32[14,8,8,16]{3,2,1,0:T(8,128)S(1)}, f32[14,8,8,16]{3,2,1,0:T(8,128)S(1)}, u32[]{:S(2)}, u32[]{:S(2)}) %collective-permute-start.27) | collective-permute-done | bytes 57376 | tf_op jit(solution)/shard_map/ppermute | solution.py:176
  175.4 3.2 collective-permute-start.28
  183.3 3.1 collective-permute-start.32
  190.7 2.2 collective-permute-done.35
  197.3 2.8 collective-permute-start.36
  209.5 2.7 collective-permute-start.40
  221.3 2.5 collective-permute-start.44
  228.8 22.5 %psum.22 = f32[]{:T(128)} all-reduce(f32[]{:T(128)} %slice_reduce_fusion.1), channel_id=1, replica_groups=mesh['tx'=4,'ty'=2,'vel'=4] {'tx','ty'}, use_global_device_ids=true, to_apply=%region_3.4 | all-reduce | flops 1 | bytes 8 | tf_op jit(solution)/shard_map/psum | solution.py:156
  257.2 2.8 convolution_add_fusion.1
  260.1 4.2 collective-permute-start.49
  264.3 5.5 %collective-permute-done.48 = f32[1,8,16,768]{3,2,1,0:T(8,128)S(1)} collective-permute-done((f32[1,8,16,768]{3,2,1,0:T(8,128)S(1)}, f32[1,8,16,768]{3,2,1,0:T(8,128)S(1)}, u32[]{:S(2)}, u32[]{:S(2)}) %collective-permute-start.48) | collective-permute-done | bytes 393248 | tf_op jit(solution)/shard_map/ppermute | solution.py:23
  269.8 2.8 collective-permute-done.49
  275.7 5.9 %collective-permute-done.50 = f32[10,1,16,768]{3,2,1,0:T(8,128)S(1)} collective-permute-done((f32[10,1,16,768]{3,2,1,0:T(8,128)S(1)}, f32[10,1,16,768]{3,2,1,0:T(8,128)S(1)}, u32[]{:S(2)}, u32[]{:S(2)}) %collective-permute-start.50) | collective-permute-done | bytes 491552 | tf_op jit(solution)/shard_map/ppermute | solution.py:23
  281.5 5.3 %collective-permute-done.51 = f32[10,1,16,768]{3,2,1,0:T(8,128)S(1)} collective-permute-done((f32[10,1,16,768]{3,2,1,0:T(8,128)S(1)}, f32[10,1,16,768]{3,2,1,0:T(8,128)S(1)}, u32[]{:S(2)}, u32[]{:S(2)}) %collective-permute-start.51) | collective-permute-done | bytes 491552 | tf_op jit(solution)/shard_map/ppermute | solution.py:25
  286.9 6.1 %multiply_select_fusion.1 = f32[8,8,16,768]{3,2,1,0:T(8,128)S(1)} fusion(f32[8,8,16,768]{3,2,1,0:T(8,128)S(1)} %convolution_add_fusion.1, f32[10,1,16,768]{3,2,1,0:T(8,128)S(1)} %collective-permute-done.51, f32[1,8,16,768]{3,2,1,0:T(8,128)S(1)} %collective-permute-done.49, f32[1,8,16,768]{3,2,1,0:T(8,128)S(1)} %collective-permute-done.48, ...), kind=kOutput, calls=%fused_computation.1 | convolution fusion | flops 73924608 | bytes 14414848 | tf_op jit(solution)/shard_map/kxyz,kv->xyzv/dot_general | solution.py:190
  293.0 11.2 %fusion.69 = f32[14,8,8,16]{3,0,2,1:T(8,128)S(1)} fusion(f32[8,8,16,768]{3,2,1,0:T(8,128)S(1)} %multiply_select_fusion.1, f32[14,768]{1,0:T(8,128)S(1)} %stack.29, f32[768]{0:T(1024)S(1)} %copy-done.8), kind=kOutput, calls=%fused_computation.579 | convolution fusion | flops 132131328 | bytes 3249152 | tf_op jit(solution)/shard_map/kv,xyzv->kxyz/dot_general | solution.py:173
  308.0 11.1 %collective-permute-done.53 = f32[14,8,8,16]{3,2,1,0:T(8,128)S(1)} collective-permute-done((f32[14,8,8,16]{3,2,1,0:T(8,128)S(1)}, f32[14,8,8,16]{3,2,1,0:T(8,128)S(1)}, u32[]{:S(2)}, u32[]{:S(2)}) %collective-permute-start.53) | collective-permute-done | bytes 57376 | tf_op jit(solution)/shard_map/ppermute | solution.py:176
  319.2 3.8 collective-permute-start.54
  327.8 3.1 collective-permute-start.58
  335.1 2.2 collective-permute-done.61
  341.7 2.8 collective-permute-start.62
  353.9 2.7 collective-permute-start.66
  365.7 2.5 collective-permute-start.70
  373.3 22.8 %psum.23 = f32[]{:T(128)} all-reduce(f32[]{:T(128)} %slice_reduce_fusion), channel_id=1, replica_groups=mesh['tx'=4,'ty'=2,'vel'=4] {'tx','ty'}, use_global_device_ids=true, to_apply=%region_5.6 | all-reduce | flops 1 | bytes 8 | tf_op jit(solution)/shard_map/psum | solution.py:156
  398.9 2.8 convolution_add_fusion
  401.9 3.8 collective-permute-start.75
  405.7 5.9 %collective-permute-done.74 = f32[1,8,16,768]{3,2,1,0:T(8,128)S(1)} collective-permute-done((f32[1,8,16,768]{3,2,1,0:T(8,128)S(1)}, f32[1,8,16,768]{3,2,1,0:T(8,128)S(1)}, u32[]{:S(2)}, u32[]{:S(2)}) %collective-permute-start.74) | collective-permute-done | bytes 393248 | tf_op jit(solution)/shard_map/ppermute | solution.py:23
  411.5 2.4 collective-permute-done.75
  417.0 5.9 %collective-permute-done.76 = f32[10,1,16,768]{3,2,1,0:T(8,128)S(1)} collective-permute-done((f32[10,1,16,768]{3,2,1,0:T(8,128)S(1)}, f32[10,1,16,768]{3,2,1,0:T(8,128)S(1)}, u32[]{:S(2)}, u32[]{:S(2)}) %collective-permute-start.76) | collective-permute-done | bytes 491552 | tf_op jit(solution)/shard_map/ppermute | solution.py:23
  422.9 5.3 %collective-permute-done.77 = f32[10,1,16,768]{3,2,1,0:T(8,128)S(1)} collective-permute-done((f32[10,1,16,768]{3,2,1,0:T(8,128)S(1)}, f32[10,1,16,768]{3,2,1,0:T(8,128)S(1)}, u32[]{:S(2)}, u32[]{:S(2)}) %collective-permute-start.77) | collective-permute-done | bytes 491552 | tf_op jit(solution)/shard_map/ppermute | solution.py:25
  428.2 7.9 %multiply_select_fusion = f32[8,8,16,768]{3,2,1,0:T(8,128)} fusion(f32[8,8,16,768]{3,2,1,0:T(8,128)S(1)} %convolution_add_fusion, f32[10,1,16,768]{3,2,1,0:T(8,128)S(1)} %collective-permute-done.77, f32[1,8,16,768]{3,2,1,0:T(8,128)S(1)} %collective-permute-done.75, f32[1,8,16,768]{3,2,1,0:T(8,128)S(1)} %collective-permute-done.74, ...), kind=kOutput, calls=%fused_computation | convolution fusion | flops 73924608 | bytes 14414848 | tf_op jit(solution)/shard_map/kxyz,kv->xyzv/dot_general | solution.py:190
  (422 shorter events, 147.3 us)
Async XLA Ops:
  19.7 13.7 %collective-permute-start.1 = (f32[14,8,8,16]{3,2,1,0:T(8,128)S(1)}, f32[14,8,8,16]{3,2,1,0:T(8,128)S(1)}, u32[]{:S(2)}, u32[]{:S(2)}) collective-permute-start(f32[14,8,8,16]{3,2,1,0:T(8,128)S(1)} %copy_add_fusion.2), channel_id=1, source_target_pairs={{0,2},{1,3},{2,0},{3,1},{4,6},{5,7},{6,4},{7,5},{8,10},{9,11},{10,... | collective-permute-start | bytes 172040 | tf_op jit(solution)/shard_map/ppermute | solution.py:176
  33.5 5.8 %collective-permute-start.3 = (f32[5,1,8,16]{3,2,1,0:T(8,128)S(1)}, f32[5,1,8,16]{3,2,1,0:T(8,128)S(1)}, u32[]{:S(2)}, u32[]{:S(2)}) collective-permute-start(f32[5,1,8,16]{3,2,1,0:T(8,128)S(1)} %get-tuple-element.84), channel_id=1, source_target_pairs={{0,8},{8,16},{16,24},{24,0},{1,9},{9,17},{17,25},{25,1},{2,10},{10... | collective-permute-start | bytes 7688 | tf_op jit(solution)/shard_map/ppermute | solution.py:23
  39.4 6.1 %collective-permute-start.5 = (f32[5,10,1,16]{3,2,1,0:T(1,128)S(1)}, f32[5,10,1,16]{3,2,1,0:T(1,128)S(1)}, u32[]{:S(2)}, u32[]{:S(2)}) collective-permute-start(f32[5,10,1,16]{3,2,1,0:T(1,128)S(1)} %get-tuple-element.162), channel_id=1, source_target_pairs={{0,4},{4,0},{1,5},{5,1},{2,6},{6,2},{3,7},{7,3},{8,12},{12,8},{9,1... | collective-permute-start | bytes 9608 | tf_op jit(solution)/shard_map/ppermute | solution.py:23
  41.5 6.1 %collective-permute-start.7 = (f32[13,1,8,16]{3,2,1,0:T(8,128)S(1)}, f32[13,1,8,16]{3,2,1,0:T(8,128)S(1)}, u32[]{:S(2)}, u32[]{:S(2)}) collective-permute-start(f32[13,1,8,16]{3,2,1,0:T(8,128)S(1)} %get-tuple-element.90), channel_id=1, source_target_pairs={{0,8},{8,16},{16,24},{24,0},{1,9},{9,17},{17,25},{25,1},{2,10},{10... | collective-permute-start | bytes 19976 | tf_op jit(solution)/shard_map/ppermute | solution.py:23
  42.9 4.9 %collective-permute-start.6 = (f32[13,1,8,16]{3,2,1,0:T(8,128)S(1)}, f32[13,1,8,16]{3,2,1,0:T(8,128)S(1)}, u32[]{:S(2)}, u32[]{:S(2)}) collective-permute-start(f32[13,1,8,16]{3,2,1,0:T(8,128)S(1)} %get-tuple-element.91), channel_id=1, source_target_pairs={{8,0},{16,8},{24,16},{0,24},{9,1},{17,9},{25,17},{1,25},{10,2},{18... | collective-permute-start | bytes 19976 | tf_op jit(solution)/shard_map/ppermute | solution.py:25
  56.1 5.6 %collective-permute-start.11 = (f32[5,1,8,16]{3,2,1,0:T(8,128)S(1)}, f32[5,1,8,16]{3,2,1,0:T(8,128)S(1)}, u32[]{:S(2)}, u32[]{:S(2)}) collective-permute-start(f32[5,1,8,16]{3,2,1,0:T(8,128)S(1)} %get-tuple-element.184), channel_id=1, source_target_pairs={{0,8},{8,16},{16,24},{24,0},{1,9},{9,17},{17,25},{25,1},{2,10},{10... | collective-permute-start | bytes 7688 | tf_op jit(solution)/shard_map/ppermute | solution.py:23
  67.6 5.7 %collective-permute-start.15 = (f32[5,1,8,16]{3,2,1,0:T(8,128)S(1)}, f32[5,1,8,16]{3,2,1,0:T(8,128)S(1)}, u32[]{:S(2)}, u32[]{:S(2)}) collective-permute-start(f32[5,1,8,16]{3,2,1,0:T(8,128)S(1)} %get-tuple-element.182), channel_id=1, source_target_pairs={{0,8},{8,16},{16,24},{24,0},{1,9},{9,17},{17,25},{25,1},{2,10},{10... | collective-permute-start | bytes 7688 | tf_op jit(solution)/shard_map/ppermute | solution.py:23
  79.6 5.7 %collective-permute-start.19 = (f32[5,1,8,16]{3,2,1,0:T(8,128)S(1)}, f32[5,1,8,16]{3,2,1,0:T(8,128)S(1)}, u32[]{:S(2)}, u32[]{:S(2)}) collective-permute-start(f32[5,1,8,16]{3,2,1,0:T(8,128)S(1)} %get-tuple-element.180), channel_id=1, source_target_pairs={{0,8},{8,16},{16,24},{24,0},{1,9},{9,17},{17,25},{25,1},{2,10},{10... | collective-permute-start | bytes 7688 | tf_op jit(solution)/shard_map/ppermute | solution.py:23
  85.4 25.4 %collective-permute-start.21 = (f32[5,10,1,16]{3,2,1,0:T(1,128)S(1)}, f32[5,10,1,16]{3,2,1,0:T(1,128)S(1)}, u32[]{:S(2)}, u32[]{:S(2)}) collective-permute-start(f32[5,10,1,16]{3,2,1,0:T(1,128)S(1)} %get-tuple-element.150), channel_id=1, source_target_pairs={{0,4},{4,0},{1,5},{5,1},{2,6},{6,2},{3,7},{7,3},{8,12},{12,8},{9,1... | collective-permute-start | bytes 9608 | tf_op jit(solution)/shard_map/ppermute | solution.py:23
  86.2 24.6 %collective-permute-start.20 = (f32[5,10,1,16]{3,2,1,0:T(1,128)S(1)}, f32[5,10,1,16]{3,2,1,0:T(1,128)S(1)}, u32[]{:S(2)}, u32[]{:S(2)}) collective-permute-start(f32[5,10,1,16]{3,2,1,0:T(1,128)S(1)} %get-tuple-element.151), channel_id=1, source_target_pairs={{4,0},{0,4},{5,1},{1,5},{6,2},{2,6},{7,3},{3,7},{12,8},{8,12},{13,... | collective-permute-start | bytes 9608 | tf_op jit(solution)/shard_map/ppermute | solution.py:25
  115.7 9.7 %collective-permute-start.22 = (f32[1,8,16,768]{3,2,1,0:T(8,128)S(1)}, f32[1,8,16,768]{3,2,1,0:T(8,128)S(1)}, u32[]{:S(2)}, u32[]{:S(2)}) collective-permute-start(f32[1,8,16,768]{3,2,1,0:T(8,128)S(1)} %get-tuple-element.60), channel_id=1, source_target_pairs={{0,8},{8,16},{16,24},{24,0},{1,9},{9,17},{17,25},{25,1},{2,10},{10... | collective-permute-start | bytes 1179656 | tf_op jit(solution)/shard_map/ppermute | solution.py:23
  115.7 12.4 %collective-permute-start.23 = (f32[1,8,16,768]{3,2,1,0:T(8,128)S(1)}, f32[1,8,16,768]{3,2,1,0:T(8,128)S(1)}, u32[]{:S(2)}, u32[]{:S(2)}) collective-permute-start(f32[1,8,16,768]{3,2,1,0:T(8,128)S(1)} %get-tuple-element.61), channel_id=1, source_target_pairs={{8,0},{16,8},{24,16},{0,24},{9,1},{17,9},{25,17},{1,25},{10,2},{18... | collective-permute-start | bytes 1179656 | tf_op jit(solution)/shard_map/ppermute | solution.py:25
  128.3 8.9 %collective-permute-start.24 = (f32[10,1,16,768]{3,2,1,0:T(8,128)S(1)}, f32[10,1,16,768]{3,2,1,0:T(8,128)S(1)}, u32[]{:S(2)}, u32[]{:S(2)}) collective-permute-start(f32[10,1,16,768]{3,2,1,0:T(8,128)S(1)} %get-tuple-element.42), channel_id=1, source_target_pairs={{0,4},{4,0},{1,5},{5,1},{2,6},{6,2},{3,7},{7,3},{8,12},{12,8},{9,1... | collective-permute-start | bytes 1474568 | tf_op jit(solution)/shard_map/ppermute | solution.py:23
  128.3 14.1 %collective-permute-start.25 = (f32[10,1,16,768]{3,2,1,0:T(8,128)S(1)}, f32[10,1,16,768]{3,2,1,0:T(8,128)S(1)}, u32[]{:S(2)}, u32[]{:S(2)}) collective-permute-start(f32[10,1,16,768]{3,2,1,0:T(8,128)S(1)} %get-tuple-element.43), channel_id=1, source_target_pairs={{4,0},{0,4},{5,1},{1,5},{6,2},{2,6},{7,3},{3,7},{12,8},{8,12},{13,... | collective-permute-start | bytes 1474568 | tf_op jit(solution)/shard_map/ppermute | solution.py:25
  162.0 12.6 %collective-permute-start.27 = (f32[14,8,8,16]{3,2,1,0:T(8,128)S(1)}, f32[14,8,8,16]{3,2,1,0:T(8,128)S(1)}, u32[]{:S(2)}, u32[]{:S(2)}) collective-permute-start(f32[14,8,8,16]{3,2,1,0:T(8,128)S(1)} %copy_add_fusion.1), channel_id=1, source_target_pairs={{0,2},{1,3},{2,0},{3,1},{4,6},{5,7},{6,4},{7,5},{8,10},{9,11},{10,... | collective-permute-start | bytes 172040 | tf_op jit(solution)/shard_map/ppermute | solution.py:176
  174.7 5.6 %collective-permute-start.29 = (f32[5,1,8,16]{3,2,1,0:T(8,128)S(1)}, f32[5,1,8,16]{3,2,1,0:T(8,128)S(1)}, u32[]{:S(2)}, u32[]{:S(2)}) collective-permute-start(f32[5,1,8,16]{3,2,1,0:T(8,128)S(1)} %get-tuple-element.82), channel_id=1, source_target_pairs={{0,8},{8,16},{16,24},{24,0},{1,9},{9,17},{17,25},{25,1},{2,10},{10... | collective-permute-start | bytes 7688 | tf_op jit(solution)/shard_map/ppermute | solution.py:23
  175.4 4.9 %collective-permute-start.28 = (f32[5,1,8,16]{3,2,1,0:T(8,128)S(1)}, f32[5,1,8,16]{3,2,1,0:T(8,128)S(1)}, u32[]{:S(2)}, u32[]{:S(2)}) collective-permute-start(f32[5,1,8,16]{3,2,1,0:T(8,128)S(1)} %get-tuple-element.83), channel_id=1, source_target_pairs={{8,0},{16,8},{24,16},{0,24},{9,1},{17,9},{25,17},{1,25},{10,2},{18... | collective-permute-start | bytes 7688 | tf_op jit(solution)/shard_map/ppermute | solution.py:25
  180.4 6.0 %collective-permute-start.31 = (f32[5,10,1,16]{3,2,1,0:T(1,128)S(1)}, f32[5,10,1,16]{3,2,1,0:T(1,128)S(1)}, u32[]{:S(2)}, u32[]{:S(2)}) collective-permute-start(f32[5,10,1,16]{3,2,1,0:T(1,128)S(1)} %get-tuple-element.146), channel_id=1, source_target_pairs={{0,4},{4,0},{1,5},{5,1},{2,6},{6,2},{3,7},{7,3},{8,12},{12,8},{9,1... | collective-permute-start | bytes 9608 | tf_op jit(solution)/shard_map/ppermute | solution.py:23
  180.5 6.0 %collective-permute-start.30 = (f32[5,10,1,16]{3,2,1,0:T(1,128)S(1)}, f32[5,10,1,16]{3,2,1,0:T(1,128)S(1)}, u32[]{:S(2)}, u32[]{:S(2)}) collective-permute-start(f32[5,10,1,16]{3,2,1,0:T(1,128)S(1)} %get-tuple-element.147), channel_id=1, source_target_pairs={{4,0},{0,4},{5,1},{1,5},{6,2},{2,6},{7,3},{3,7},{12,8},{8,12},{13,... | collective-permute-start | bytes 9608 | tf_op jit(solution)/shard_map/ppermute | solution.py:25
  182.5 6.0 %collective-permute-start.33 = (f32[13,1,8,16]{3,2,1,0:T(8,128)S(1)}, f32[13,1,8,16]{3,2,1,0:T(8,128)S(1)}, u32[]{:S(2)}, u32[]{:S(2)}) collective-permute-start(f32[13,1,8,16]{3,2,1,0:T(8,128)S(1)} %get-tuple-element.88), channel_id=1, source_target_pairs={{0,8},{8,16},{16,24},{24,0},{1,9},{9,17},{17,25},{25,1},{2,10},{10... | collective-permute-start | bytes 19976 | tf_op jit(solution)/shard_map/ppermute | solution.py:23
  183.3 5.2 %collective-permute-start.32 = (f32[13,1,8,16]{3,2,1,0:T(8,128)S(1)}, f32[13,1,8,16]{3,2,1,0:T(8,128)S(1)}, u32[]{:S(2)}, u32[]{:S(2)}) collective-permute-start(f32[13,1,8,16]{3,2,1,0:T(8,128)S(1)} %get-tuple-element.89), channel_id=1, source_target_pairs={{8,0},{16,8},{24,16},{0,24},{9,1},{17,9},{25,17},{1,25},{10,2},{18... | collective-permute-start | bytes 19976 | tf_op jit(solution)/shard_map/ppermute | solution.py:25
  188.8 4.9 %collective-permute-start.34 = (f32[13,10,1,16]{3,2,1,0:T(1,128)S(1)}, f32[13,10,1,16]{3,2,1,0:T(1,128)S(1)}, u32[]{:S(2)}, u32[]{:S(2)}) collective-permute-start(f32[13,10,1,16]{3,2,1,0:T(1,128)S(1)} %get-tuple-element.75), channel_id=1, source_target_pairs={{4,0},{0,4},{5,1},{1,5},{6,2},{2,6},{7,3},{3,7},{12,8},{8,12},{13,... | collective-permute-start | bytes 24968 | tf_op jit(solution)/shard_map/ppermute | solution.py:25
  196.1 5.7 %collective-permute-start.37 = (f32[5,1,8,16]{3,2,1,0:T(8,128)S(1)}, f32[5,1,8,16]{3,2,1,0:T(8,128)S(1)}, u32[]{:S(2)}, u32[]{:S(2)}) collective-permute-start(f32[5,1,8,16]{3,2,1,0:T(8,128)S(1)} %get-tuple-element.176), channel_id=1, source_target_pairs={{0,8},{8,16},{16,24},{24,0},{1,9},{9,17},{17,25},{25,1},{2,10},{10... | collective-permute-start | bytes 7688 | tf_op jit(solution)/shard_map/ppermute | solution.py:23
  208.2 5.7 %collective-permute-start.41 = (f32[5,1,8,16]{3,2,1,0:T(8,128)S(1)}, f32[5,1,8,16]{3,2,1,0:T(8,128)S(1)}, u32[]{:S(2)}, u32[]{:S(2)}) collective-permute-start(f32[5,1,8,16]{3,2,1,0:T(8,128)S(1)} %get-tuple-element.174), channel_id=1, source_target_pairs={{0,8},{8,16},{16,24},{24,0},{1,9},{9,17},{17,25},{25,1},{2,10},{10... | collective-permute-start | bytes 7688 | tf_op jit(solution)/shard_map/ppermute | solution.py:23
  219.7 5.8 %collective-permute-start.45 = (f32[5,1,8,16]{3,2,1,0:T(8,128)S(1)}, f32[5,1,8,16]{3,2,1,0:T(8,128)S(1)}, u32[]{:S(2)}, u32[]{:S(2)}) collective-permute-start(f32[5,1,8,16]{3,2,1,0:T(8,128)S(1)} %get-tuple-element.172), channel_id=1, source_target_pairs={{0,8},{8,16},{16,24},{24,0},{1,9},{9,17},{17,25},{25,1},{2,10},{10... | collective-permute-start | bytes 7688 | tf_op jit(solution)/shard_map/ppermute | solution.py:23
  226.2 25.7 %collective-permute-start.47 = (f32[5,10,1,16]{3,2,1,0:T(1,128)}, f32[5,10,1,16]{3,2,1,0:T(1,128)}, u32[]{:S(2)}, u32[]{:S(2)}) collective-permute-start(f32[5,10,1,16]{3,2,1,0:T(1,128)} %get-tuple-element.134), channel_id=1, source_target_pairs={{0,4},{4,0},{1,5},{5,1},{2,6},{6,2},{3,7},{7,3},{8,12},{12,8},{9,1... | collective-permute-start | bytes 9608 | tf_op jit(solution)/shard_map/ppermute | solution.py:23
  227.4 24.5 %collective-permute-start.46 = (f32[5,10,1,16]{3,2,1,0:T(1,128)}, f32[5,10,1,16]{3,2,1,0:T(1,128)}, u32[]{:S(2)}, u32[]{:S(2)}) collective-permute-start(f32[5,10,1,16]{3,2,1,0:T(1,128)} %get-tuple-element.135), channel_id=1, source_target_pairs={{4,0},{0,4},{5,1},{1,5},{6,2},{2,6},{7,3},{3,7},{12,8},{8,12},{13,... | collective-permute-start | bytes 9608 | tf_op jit(solution)/shard_map/ppermute | solution.py:25
  260.0 9.7 %collective-permute-start.48 = (f32[1,8,16,768]{3,2,1,0:T(8,128)S(1)}, f32[1,8,16,768]{3,2,1,0:T(8,128)S(1)}, u32[]{:S(2)}, u32[]{:S(2)}) collective-permute-start(f32[1,8,16,768]{3,2,1,0:T(8,128)S(1)} %get-tuple-element.54), channel_id=1, source_target_pairs={{0,8},{8,16},{16,24},{24,0},{1,9},{9,17},{17,25},{25,1},{2,10},{10... | collective-permute-start | bytes 1179656 | tf_op jit(solution)/shard_map/ppermute | solution.py:23
  260.1 12.4 %collective-permute-start.49 = (f32[1,8,16,768]{3,2,1,0:T(8,128)S(1)}, f32[1,8,16,768]{3,2,1,0:T(8,128)S(1)}, u32[]{:S(2)}, u32[]{:S(2)}) collective-permute-start(f32[1,8,16,768]{3,2,1,0:T(8,128)S(1)} %get-tuple-element.55), channel_id=1, source_target_pairs={{8,0},{16,8},{24,16},{0,24},{9,1},{17,9},{25,17},{1,25},{10,2},{18... | collective-permute-start | bytes 1179656 | tf_op jit(solution)/shard_map/ppermute | solution.py:25
  272.6 8.9 %collective-permute-start.50 = (f32[10,1,16,768]{3,2,1,0:T(8,128)S(1)}, f32[10,1,16,768]{3,2,1,0:T(8,128)S(1)}, u32[]{:S(2)}, u32[]{:S(2)}) collective-permute-start(f32[10,1,16,768]{3,2,1,0:T(8,128)S(1)} %get-tuple-element.40), channel_id=1, source_target_pairs={{0,4},{4,0},{1,5},{5,1},{2,6},{6,2},{3,7},{7,3},{8,12},{12,8},{9,1... | collective-permute-start | bytes 1474568 | tf_op jit(solution)/shard_map/ppermute | solution.py:23
  272.7 14.1 %collective-permute-start.51 = (f32[10,1,16,768]{3,2,1,0:T(8,128)S(1)}, f32[10,1,16,768]{3,2,1,0:T(8,128)S(1)}, u32[]{:S(2)}, u32[]{:S(2)}) collective-permute-start(f32[10,1,16,768]{3,2,1,0:T(8,128)S(1)} %get-tuple-element.41), channel_id=1, source_target_pairs={{4,0},{0,4},{5,1},{1,5},{6,2},{2,6},{7,3},{3,7},{12,8},{8,12},{13,... | collective-permute-start | bytes 1474568 | tf_op jit(solution)/shard_map/ppermute | solution.py:25
  306.4 12.6 %collective-permute-start.53 = (f32[14,8,8,16]{3,2,1,0:T(8,128)S(1)}, f32[14,8,8,16]{3,2,1,0:T(8,128)S(1)}, u32[]{:S(2)}, u32[]{:S(2)}) collective-permute-start(f32[14,8,8,16]{3,2,1,0:T(8,128)S(1)} %copy_add_fusion), channel_id=1, source_target_pairs={{0,2},{1,3},{2,0},{3,1},{4,6},{5,7},{6,4},{7,5},{8,10},{9,11},{10,... | collective-permute-start | bytes 172040 | tf_op jit(solution)/shard_map/ppermute | solution.py:176
  319.1 5.6 %collective-permute-start.55 = (f32[5,1,8,16]{3,2,1,0:T(8,128)S(1)}, f32[5,1,8,16]{3,2,1,0:T(8,128)S(1)}, u32[]{:S(2)}, u32[]{:S(2)}) collective-permute-start(f32[5,1,8,16]{3,2,1,0:T(8,128)S(1)} %get-tuple-element.80), channel_id=1, source_target_pairs={{0,8},{8,16},{16,24},{24,0},{1,9},{9,17},{17,25},{25,1},{2,10},{10... | collective-permute-start | bytes 7688 | tf_op jit(solution)/shard_map/ppermute | solution.py:23
  319.2 5.6 %collective-permute-start.54 = (f32[5,1,8,16]{3,2,1,0:T(8,128)S(1)}, f32[5,1,8,16]{3,2,1,0:T(8,128)S(1)}, u32[]{:S(2)}, u32[]{:S(2)}) collective-permute-start(f32[5,1,8,16]{3,2,1,0:T(8,128)S(1)} %get-tuple-element.81), channel_id=1, source_target_pairs={{8,0},{16,8},{24,16},{0,24},{9,1},{17,9},{25,17},{1,25},{10,2},{18... | collective-permute-start | bytes 7688 | tf_op jit(solution)/shard_map/ppermute | solution.py:25
  324.8 6.0 %collective-permute-start.57 = (f32[5,10,1,16]{3,2,1,0:T(1,128)S(1)}, f32[5,10,1,16]{3,2,1,0:T(1,128)S(1)}, u32[]{:S(2)}, u32[]{:S(2)}) collective-permute-start(f32[5,10,1,16]{3,2,1,0:T(1,128)S(1)} %get-tuple-element.130), channel_id=1, source_target_pairs={{0,4},{4,0},{1,5},{5,1},{2,6},{6,2},{3,7},{7,3},{8,12},{12,8},{9,1... | collective-permute-start | bytes 9608 | tf_op jit(solution)/shard_map/ppermute | solution.py:23
  324.9 6.0 %collective-permute-start.56 = (f32[5,10,1,16]{3,2,1,0:T(1,128)S(1)}, f32[5,10,1,16]{3,2,1,0:T(1,128)S(1)}, u32[]{:S(2)}, u32[]{:S(2)}) collective-permute-start(f32[5,10,1,16]{3,2,1,0:T(1,128)S(1)} %get-tuple-element.131), channel_id=1, source_target_pairs={{4,0},{0,4},{5,1},{1,5},{6,2},{2,6},{7,3},{3,7},{12,8},{8,12},{13,... | collective-permute-start | bytes 9608 | tf_op jit(solution)/shard_map/ppermute | solution.py:25
  326.9 6.0 %collective-permute-start.59 = (f32[13,1,8,16]{3,2,1,0:T(8,128)S(1)}, f32[13,1,8,16]{3,2,1,0:T(8,128)S(1)}, u32[]{:S(2)}, u32[]{:S(2)}) collective-permute-start(f32[13,1,8,16]{3,2,1,0:T(8,128)S(1)} %get-tuple-element.86), channel_id=1, source_target_pairs={{0,8},{8,16},{16,24},{24,0},{1,9},{9,17},{17,25},{25,1},{2,10},{10... | collective-permute-start | bytes 19976 | tf_op jit(solution)/shard_map/ppermute | solution.py:23
  327.8 5.2 %collective-permute-start.58 = (f32[13,1,8,16]{3,2,1,0:T(8,128)S(1)}, f32[13,1,8,16]{3,2,1,0:T(8,128)S(1)}, u32[]{:S(2)}, u32[]{:S(2)}) collective-permute-start(f32[13,1,8,16]{3,2,1,0:T(8,128)S(1)} %get-tuple-element.87), channel_id=1, source_target_pairs={{8,0},{16,8},{24,16},{0,24},{9,1},{17,9},{25,17},{1,25},{10,2},{18... | collective-permute-start | bytes 19976 | tf_op jit(solution)/shard_map/ppermute | solution.py:25
  333.2 4.9 %collective-permute-start.60 = (f32[13,10,1,16]{3,2,1,0:T(1,128)S(1)}, f32[13,10,1,16]{3,2,1,0:T(1,128)S(1)}, u32[]{:S(2)}, u32[]{:S(2)}) collective-permute-start(f32[13,10,1,16]{3,2,1,0:T(1,128)S(1)} %get-tuple-element.71), channel_id=1, source_target_pairs={{4,0},{0,4},{5,1},{1,5},{6,2},{2,6},{7,3},{3,7},{12,8},{8,12},{13,... | collective-permute-start | bytes 24968 | tf_op jit(solution)/shard_map/ppermute | solution.py:25
  340.5 5.7 %collective-permute-start.63 = (f32[5,1,8,16]{3,2,1,0:T(8,128)S(1)}, f32[5,1,8,16]{3,2,1,0:T(8,128)S(1)}, u32[]{:S(2)}, u32[]{:S(2)}) collective-permute-start(f32[5,1,8,16]{3,2,1,0:T(8,128)S(1)} %get-tuple-element.168), channel_id=1, source_target_pairs={{0,8},{8,16},{16,24},{24,0},{1,9},{9,17},{17,25},{25,1},{2,10},{10... | collective-permute-start | bytes 7688 | tf_op jit(solution)/shard_map/ppermute | solution.py:23
  352.6 5.7 %collective-permute-start.67 = (f32[5,1,8,16]{3,2,1,0:T(8,128)S(1)}, f32[5,1,8,16]{3,2,1,0:T(8,128)S(1)}, u32[]{:S(2)}, u32[]{:S(2)}) collective-permute-start(f32[5,1,8,16]{3,2,1,0:T(8,128)S(1)} %get-tuple-element.166), channel_id=1, source_target_pairs={{0,8},{8,16},{16,24},{24,0},{1,9},{9,17},{17,25},{25,1},{2,10},{10... | collective-permute-start | bytes 7688 | tf_op jit(solution)/shard_map/ppermute | solution.py:23
  364.1 5.8 %collective-permute-start.71 = (f32[5,1,8,16]{3,2,1,0:T(8,128)S(1)}, f32[5,1,8,16]{3,2,1,0:T(8,128)S(1)}, u32[]{:S(2)}, u32[]{:S(2)}) collective-permute-start(f32[5,1,8,16]{3,2,1,0:T(8,128)S(1)} %get-tuple-element.164), channel_id=1, source_target_pairs={{0,8},{8,16},{16,24},{24,0},{1,9},{9,17},{17,25},{25,1},{2,10},{10... | collective-permute-start | bytes 7688 | tf_op jit(solution)/shard_map/ppermute | solution.py:23
  370.6 26.2 %collective-permute-start.73 = (f32[5,10,1,16]{3,2,1,0:T(1,128)}, f32[5,10,1,16]{3,2,1,0:T(1,128)S(1)}, u32[]{:S(2)}, u32[]{:S(2)}) collective-permute-start(f32[5,10,1,16]{3,2,1,0:T(1,128)} %get-tuple-element.118), channel_id=1, source_target_pairs={{0,4},{4,0},{1,5},{5,1},{2,6},{6,2},{3,7},{7,3},{8,12},{12,8},{9,1... | collective-permute-start | bytes 9608 | tf_op jit(solution)/shard_map/ppermute | solution.py:23
  371.8 25.0 %collective-permute-start.72 = (f32[5,10,1,16]{3,2,1,0:T(1,128)}, f32[5,10,1,16]{3,2,1,0:T(1,128)S(1)}, u32[]{:S(2)}, u32[]{:S(2)}) collective-permute-start(f32[5,10,1,16]{3,2,1,0:T(1,128)} %get-tuple-element.119), channel_id=1, source_target_pairs={{4,0},{0,4},{5,1},{1,5},{6,2},{2,6},{7,3},{3,7},{12,8},{8,12},{13,... | collective-permute-start | bytes 9608 | tf_op jit(solution)/shard_map/ppermute | solution.py:25
  401.8 9.7 %collective-permute-start.74 = (f32[1,8,16,768]{3,2,1,0:T(8,128)S(1)}, f32[1,8,16,768]{3,2,1,0:T(8,128)S(1)}, u32[]{:S(2)}, u32[]{:S(2)}) collective-permute-start(f32[1,8,16,768]{3,2,1,0:T(8,128)S(1)} %get-tuple-element.48), channel_id=1, source_target_pairs={{0,8},{8,16},{16,24},{24,0},{1,9},{9,17},{17,25},{25,1},{2,10},{10... | collective-permute-start | bytes 1179656 | tf_op jit(solution)/shard_map/ppermute | solution.py:23
  401.9 12.0 %collective-permute-start.75 = (f32[1,8,16,768]{3,2,1,0:T(8,128)S(1)}, f32[1,8,16,768]{3,2,1,0:T(8,128)S(1)}, u32[]{:S(2)}, u32[]{:S(2)}) collective-permute-start(f32[1,8,16,768]{3,2,1,0:T(8,128)S(1)} %get-tuple-element.49), channel_id=1, source_target_pairs={{8,0},{16,8},{24,16},{0,24},{9,1},{17,9},{25,17},{1,25},{10,2},{18... | collective-permute-start | bytes 1179656 | tf_op jit(solution)/shard_map/ppermute | solution.py:25
  414.0 8.9 %collective-permute-start.76 = (f32[10,1,16,768]{3,2,1,0:T(8,128)S(1)}, f32[10,1,16,768]{3,2,1,0:T(8,128)S(1)}, u32[]{:S(2)}, u32[]{:S(2)}) collective-permute-start(f32[10,1,16,768]{3,2,1,0:T(8,128)S(1)} %get-tuple-element.38), channel_id=1, source_target_pairs={{0,4},{4,0},{1,5},{5,1},{2,6},{6,2},{3,7},{7,3},{8,12},{12,8},{9,1... | collective-permute-start | bytes 1474568 | tf_op jit(solution)/shard_map/ppermute | solution.py:23
  414.1 14.1 %collective-permute-start.77 = (f32[10,1,16,768]{3,2,1,0:T(8,128)S(1)}, f32[10,1,16,768]{3,2,1,0:T(8,128)S(1)}, u32[]{:S(2)}, u32[]{:S(2)}) collective-permute-start(f32[10,1,16,768]{3,2,1,0:T(8,128)S(1)} %get-tuple-element.39), channel_id=1, source_target_pairs={{4,0},{0,4},{5,1},{1,5},{6,2},{2,6},{7,3},{3,7},{12,8},{8,12},{13,... | collective-permute-start | bytes 1474568 | tf_op jit(solution)/shard_map/ppermute | solution.py:25
  (67 other events, 1016.8 us)
